TPU v7x, 256 devices: a whole 4x4x8 slice. The times are simulated.
256 devices in a mesh: ctx: 32 (over z, y_hi, core), kvh: 8 (over x, y_lo).
Axes of the slice: x: 4, y: 4 (y_hi: 2, y_lo: 2; y = y_hi * 2 + y_lo), z: 8, core: 2. Of those that a mesh axis runs over, the one named last changes fastest.
Arguments:
- queries: bfloat16 [4096, 8192], P('ctx', 'kvh'), may hold values from -40 to 40
- cache_keys: bfloat16 [16384, 1024], P('ctx', 'kvh'), may hold values from -6 to 6
- cache_values: bfloat16 [16384, 1024], P('ctx', 'kvh'), may hold values from -6 to 6
- new_keys: bfloat16 [4096, 1024], P('ctx', 'kvh'), may hold values from -6 to 6
- new_values: bfloat16 [4096, 1024], P('ctx', 'kvh'), may hold values from -6 to 6
- cache_fill: int32 [32], replicated, may hold values from 1 to 512, 8192 in all
- span_pos: int32 [32], P('ctx'), may hold values from 0 to 511
- destination: int32 [32], replicated, may hold values from 0 to 31, each once
Outputs:
- attn_out: bfloat16 [4096, 8192], P(('ctx', 'kvh'))
- appended_keys: bfloat16 [4096, 1024], P('ctx', 'kvh')
- appended_values: bfloat16 [4096, 1024], P('ctx', 'kvh')
Inputs may be any that keep to these rules, and one draw needn't show every extreme that they name: `cache_fill`: every shard has at least one live token; the counts sum to 8192. `destination`: each slot is named by exactly one span.
All inputs are finite; a program needn't handle non-finite values.
Results may differ from a plain program's by a relative error of at most 0.007.
Values may be sent and summed in bfloat16 or wider, within the bound.
A program may use at most 64 MiB of HBM per device.

v0:
```python
import jax
import jax.numpy as jnp
from jax import lax
from jax.sharding import PartitionSpec as P

SPAN = 128
HOPS = 8


masked_score = -1e30


def passed_along(array, axis, by):
    size = lax.axis_size(axis)
    return lax.ppermute(array, axis, [(i, (i + by) % size) for i in range(size)])


def side_by_side(arrays, axis, dim, along):
    ends, at = ([], 0)
    for a in arrays[:-1]:
        at += a.shape[along]
        ends.append(at)
    both = jnp.concatenate(arrays, axis=along)
    return tuple(jnp.split(lax.all_gather(both, axis, axis=dim, tiled=True), ends, axis=along))


def absorb(carry_state, query, key_rows, value_rows, visible, scaling):
    accum, running_max, denominator = carry_state
    scores = (
        jnp.einsum("rgd,kd->rgk", query, key_rows, preferred_element_type=jnp.float32) * scaling
    )
    scores = jnp.where(visible[:, None, :], scores, masked_score)
    new_max = jnp.maximum(running_max, jnp.max(scores, axis=2))
    factor = jnp.exp(running_max - new_max)
    weights = jnp.where(visible[:, None, :], jnp.exp(scores - new_max[:, :, None]), 0.0)
    denominator = denominator * factor + jnp.sum(weights, axis=2)
    packed = weights.astype(jnp.bfloat16)
    accum = accum * factor[:, :, None] + jnp.einsum(
        "rgk,kd->rgd", packed, value_rows, preferred_element_type=jnp.float32
    )
    return (accum, new_max, denominator)


def absorb_shard(carry_state, query, key_rows, value_rows, live_count, limit_rows, scaling):
    slot_count = key_rows.shape[0]
    block_size = min(slot_count, 256)
    block_count = slot_count // block_size
    key_blocks = key_rows.reshape(block_count, block_size, key_rows.shape[1])
    value_blocks = value_rows.reshape(block_count, block_size, value_rows.shape[1])
    block_starts = jnp.arange(block_count, dtype=jnp.int32) * block_size

    def one_block(inner_state, pieces):
        key_block, value_block, block_start = pieces
        positions = block_start + jnp.arange(block_size, dtype=jnp.int32)
        visible = (positions[None, :] < live_count) & (positions[None, :] <= limit_rows[:, None])
        return (absorb(inner_state, query, key_block, value_block, visible, scaling), None)

    carry_state, unused = lax.scan(one_block, carry_state, (key_blocks, value_blocks, block_starts))
    return carry_state


def per_device(
    queries, cache_keys, cache_values, new_keys, new_values, cache_fill, span_pos, destination
):
    row_count = queries.shape[0]
    head_dim = cache_keys.shape[1]
    group_count = queries.shape[1] // head_dim
    scaling = head_dim ** (-0.5)
    spans_here = row_count // SPAN
    ctx_count = lax.axis_size("ctx")
    ctx_index = lax.axis_index("ctx")
    query = queries.reshape(row_count, group_count, head_dim)
    row_ids = jnp.arange(row_count, dtype=jnp.int32)
    span_of = row_ids // SPAN
    limit_home = (span_pos[:, None] + jnp.arange(SPAN, dtype=jnp.int32)[None, :]).reshape(row_count)
    limit_far = jnp.full((row_count,), 2**30, jnp.int32)
    shard_ids = jnp.arange(ctx_count, dtype=jnp.int32)
    own_visible = (span_of[None, :] == span_of[:, None]) & (row_ids[None, :] <= row_ids[:, None])
    carry_state = (
        jnp.zeros((row_count, group_count, head_dim), jnp.float32),
        jnp.full((row_count, group_count), masked_score, jnp.float32),
        jnp.zeros((row_count, group_count), jnp.float32),
    )
    carry_state = absorb(carry_state, query, new_keys, new_values, own_visible, scaling)
    key_rows, value_rows = (cache_keys, cache_values)
    for hop_index in range(HOPS):
        if hop_index > 0:
            key_rows, value_rows = passed_along((key_rows, value_rows), "ctx", 1)
        limit_rows = limit_home if hop_index == 0 else limit_far
        shard_index = (ctx_index - hop_index) % ctx_count
        carry_state = absorb_shard(
            carry_state,
            query,
            key_rows,
            value_rows,
            jnp.sum(jnp.where(shard_ids == shard_index, cache_fill, 0)),
            limit_rows,
            scaling,
        )
    accum, running_max, denominator = carry_state
    result = (
        (accum / denominator[:, :, None])
        .astype(jnp.bfloat16)
        .reshape(row_count, group_count * head_dim)
    )
    attn_out = lax.all_to_all(result, "kvh", split_axis=0, concat_axis=1, tiled=True)
    every_keys, every_values = side_by_side((new_keys, new_values), "ctx", 0, 1)
    span_total = every_keys.shape[0] // SPAN
    slot_ids = ctx_index * spans_here + jnp.arange(spans_here, dtype=jnp.int32)
    picker = (destination[None, :] == slot_ids[:, None]).astype(jnp.bfloat16)
    appended_keys = jnp.dot(
        picker, every_keys.reshape(span_total, SPAN * head_dim), preferred_element_type=jnp.float32
    )
    appended_values = jnp.dot(
        picker,
        every_values.reshape(span_total, SPAN * head_dim),
        preferred_element_type=jnp.float32,
    )
    appended_keys = appended_keys.astype(jnp.bfloat16).reshape(row_count, head_dim)
    appended_values = appended_values.astype(jnp.bfloat16).reshape(row_count, head_dim)
    return (attn_out, appended_keys, appended_values)


def solution(mesh):
    placed = (
        P("ctx", "kvh"),
        P("ctx", "kvh"),
        P("ctx", "kvh"),
        P("ctx", "kvh"),
        P("ctx", "kvh"),
        P(),
        P("ctx"),
        P(),
    )
    return jax.shard_map(
        per_device,
        mesh=mesh,
        in_specs=placed,
        out_specs=(P(("ctx", "kvh"), None), P("ctx", "kvh"), P("ctx", "kvh")),
        check_vma=False,
    )
```

profile of v0, /device:TPU:16, one launch (start us, length us, event | category | flops | bytes accessed | tf_op | source)
XLA Modules:
  0.0 129.2 jit_solution(17717720852295984556)
XLA Ops:
  7.3 1.8 %collective-permute-start.1 = (bf16[512,128]{1,0:T(8,128)(2,1)}, bf16[512,128]{1,0:T(8,128)(2,1)}, u32[]{:S(2)}, u32[]{:S(2)}) collective-permute-start(bf16[512,128]{1,0:T(8,128)(2,1)} %param.26), channel_id=1, source_target_pairs={{0,8},{8,16},{16,24},{24,32},{32,40},{40,48},{48,56},{56,64},{64,7... | collective-permute-start | bytes 393224 | tf_op jit(solution)/shard_map/ppermute | solution.py:15
  9.1 1.4 %pad_maximum_fusion = bf16[128,256]{1,0:T(8,128)(2,1)} fusion(bf16[128,128]{1,0:T(8,128)(2,1)} %param.28, bf16[128,128]{1,0:T(8,128)(2,1)} %param.27), kind=kLoop, calls=%fused_computation.174 | loop fusion | flops 131072 | bytes 131072 | tf_op jit(solution)/shard_map/concatenate | solution.py:23
  14.5 8.5 %while.120 = (s32[]{:T(128)}, f32[128,8,128]{2,0,1:T(8,128)S(1)}, f32[128,8]{0,1:T(8,128)S(1)}, f32[128,8]{0,1:T(8,128)S(1)}, s32[2]{0:T(128)S(1)}, /*index=5*/s...) while((s32[]{:T(128)}, f32[128,8,128]{2,0,1:T(8,128)S(1)}, ...), condition=%wide.region_6.7_spmd.clone, body=%wide.region_3.6_spmd.clone.sunk | while | flops 136907648 | bytes 4787857 | solution.py:58
  23.2 3.2 %collective-permute-start.3 = (bf16[512,128]{1,0:T(8,128)(2,1)}, bf16[512,128]{1,0:T(8,128)(2,1)}, u32[]{:S(2)}, u32[]{:S(2)}) collective-permute-start(bf16[512,128]{1,0:T(8,128)(2,1)} %collective-permute-done.1), channel_id=1, source_target_pairs={{0,8},{8,16},{16,24},{24,32},{32,40},{40,48},{48,56},{56,64},{64,7... | collective-permute-start | bytes 393224 | tf_op jit(solution)/shard_map/ppermute | solution.py:15
  26.4 9.4 %while.113 = (s32[]{:T(128)}, f32[128,8,128]{2,0,1:T(8,128)S(1)}, f32[128,8]{0,1:T(8,128)S(1)}, f32[128,8]{0,1:T(8,128)S(1)}, s32[2]{0:T(128)S(1)}, /*index=5*/s...) while((s32[]{:T(128)}, f32[128,8,128]{2,0,1:T(8,128)S(1)}, ...), condition=%wide.region_11.12_spmd, body=%wide.region_8.11_spmd.sunk | while | flops 136842240 | bytes 4655225 | solution.py:58
  29.7 1.4 %convolution_add_fusion.17 = f32[128,8,128]{2,0,1:T(8,128)S(1)} fusion(f32[128,8,256]{0,2,1:T(8,128)S(1)} %get-tuple-element.1199, f32[128,8]{0,1:T(8,128)S(1)} %max.33, f32[128,8,128]{2,0,1:T(8,128)S(1)} %get-tuple-element.1339, pred[256]{0:T(512)(128)(4,1)S(1)} %compare_and_fusion.16, f32[128,8]{0,1:T(8,128)S(1)} %get-tuple-element.1201, ...), kind=kOutput, calls=%fused_computation.4.clone.1 | convolution fusion | flops 68157440 | bytes 2171648 | tf_op jit(solution)/shard_map/while/body/eval_jaxpr/rgk,kd->rgd/dot_general | solution.py:38
  34.4 1.4 %convolution_add_fusion.17 = f32[128,8,128]{2,0,1:T(8,128)S(1)} fusion(f32[128,8,256]{0,2,1:T(8,128)S(1)} %get-tuple-element.1199, f32[128,8]{0,1:T(8,128)S(1)} %max.33, f32[128,8,128]{2,0,1:T(8,128)S(1)} %get-tuple-element.1339, pred[256]{0:T(512)(128)(4,1)S(1)} %compare_and_fusion.16, f32[128,8]{0,1:T(8,128)S(1)} %get-tuple-element.1201, ...), kind=kOutput, calls=%fused_computation.4.clone.1 | convolution fusion | flops 68157440 | bytes 2171648 | tf_op jit(solution)/shard_map/while/body/eval_jaxpr/rgk,kd->rgd/dot_general | solution.py:38
  36.0 1.7 %collective-permute-start.5 = (bf16[512,128]{1,0:T(8,128)(2,1)}, bf16[512,128]{1,0:T(8,128)(2,1)}, u32[]{:S(2)}, u32[]{:S(2)}) collective-permute-start(bf16[512,128]{1,0:T(8,128)(2,1)} %collective-permute-done.3), channel_id=1, source_target_pairs={{0,8},{8,16},{16,24},{24,32},{32,40},{40,48},{48,56},{56,64},{64,7... | collective-permute-start | bytes 393224 | tf_op jit(solution)/shard_map/ppermute | solution.py:15
  37.7 9.6 %while.114 = (s32[]{:T(128)}, f32[128,8,128]{2,0,1:T(8,128)S(1)}, f32[128,8]{0,1:T(8,128)S(1)}, f32[128,8]{0,1:T(8,128)S(1)}, s32[2]{0:T(128)S(1)}, /*index=5*/s...) while((s32[]{:T(128)}, f32[128,8,128]{2,0,1:T(8,128)S(1)}, ...), condition=%wide.region_16.17_spmd, body=%wide.region_13.16_spmd.sunk | while | flops 136842240 | bytes 4655225 | solution.py:58
  41.1 1.4 %convolution_add_fusion.18 = f32[128,8,128]{2,0,1:T(8,128)S(1)} fusion(f32[128,8,256]{0,2,1:T(8,128)S(1)} %get-tuple-element.1212, f32[128,8]{0,1:T(8,128)S(1)} %max.34, f32[128,8,128]{2,0,1:T(8,128)S(1)} %get-tuple-element.1369, pred[256]{0:T(512)(128)(4,1)S(1)} %compare_and_fusion.17, f32[128,8]{0,1:T(8,128)S(1)} %get-tuple-element.1214, ...), kind=kOutput, calls=%fused_computation.24.clone.1 | convolution fusion | flops 68157440 | bytes 2171648 | tf_op jit(solution)/shard_map/while/body/eval_jaxpr/rgk,kd->rgd/dot_general | solution.py:38
  45.9 1.4 %convolution_add_fusion.18 = f32[128,8,128]{2,0,1:T(8,128)S(1)} fusion(f32[128,8,256]{0,2,1:T(8,128)S(1)} %get-tuple-element.1212, f32[128,8]{0,1:T(8,128)S(1)} %max.34, f32[128,8,128]{2,0,1:T(8,128)S(1)} %get-tuple-element.1369, pred[256]{0:T(512)(128)(4,1)S(1)} %compare_and_fusion.17, f32[128,8]{0,1:T(8,128)S(1)} %get-tuple-element.1214, ...), kind=kOutput, calls=%fused_computation.24.clone.1 | convolution fusion | flops 68157440 | bytes 2171648 | tf_op jit(solution)/shard_map/while/body/eval_jaxpr/rgk,kd->rgd/dot_general | solution.py:38
  47.5 3.2 %collective-permute-start.7 = (bf16[512,128]{1,0:T(8,128)(2,1)}, bf16[512,128]{1,0:T(8,128)(2,1)}, u32[]{:S(2)}, u32[]{:S(2)}) collective-permute-start(bf16[512,128]{1,0:T(8,128)(2,1)} %collective-permute-done.5), channel_id=1, source_target_pairs={{0,8},{8,16},{16,24},{24,32},{32,40},{40,48},{48,56},{56,64},{64,7... | collective-permute-start | bytes 393224 | tf_op jit(solution)/shard_map/ppermute | solution.py:15
  50.7 9.8 %while.115 = (s32[]{:T(128)}, f32[128,8,128]{2,0,1:T(8,128)S(1)}, f32[128,8]{0,1:T(8,128)S(1)}, f32[128,8]{0,1:T(8,128)S(1)}, s32[2]{0:T(128)S(1)}, /*index=5*/s...) while((s32[]{:T(128)}, f32[128,8,128]{2,0,1:T(8,128)S(1)}, ...), condition=%wide.region_21.22_spmd, body=%wide.region_18.21_spmd.sunk | while | flops 136842240 | bytes 4655225 | solution.py:58
  51.4 1.4 %compare_and_fusion.18 = pred[256]{0:T(512)(128)(4,1)S(1)} fusion(s32[]{:T(128)} %get-tuple-element.1413, s32[]{:T(128)} %bitcast.204), kind=kLoop, calls=%fused_computation.57.clone.1 | loop fusion | flops 1024 | bytes 264 | tf_op jit(solution)/shard_map/while/body/eval_jaxpr/and | solution.py:55
  54.2 1.4 %convolution_add_fusion.19 = f32[128,8,128]{2,0,1:T(8,128)S(1)} fusion(f32[128,8,256]{0,2,1:T(8,128)S(1)} %get-tuple-element.1225, f32[128,8]{0,1:T(8,128)S(1)} %max.35, f32[128,8,128]{2,0,1:T(8,128)S(1)} %get-tuple-element.1399, pred[256]{0:T(512)(128)(4,1)S(1)} %compare_and_fusion.18, f32[128,8]{0,1:T(8,128)S(1)} %get-tuple-element.1227, ...), kind=kOutput, calls=%fused_computation.44.clone.1 | convolution fusion | flops 68157440 | bytes 2171648 | tf_op jit(solution)/shard_map/while/body/eval_jaxpr/rgk,kd->rgd/dot_general | solution.py:38
  59.1 1.4 %convolution_add_fusion.19 = f32[128,8,128]{2,0,1:T(8,128)S(1)} fusion(f32[128,8,256]{0,2,1:T(8,128)S(1)} %get-tuple-element.1225, f32[128,8]{0,1:T(8,128)S(1)} %max.35, f32[128,8,128]{2,0,1:T(8,128)S(1)} %get-tuple-element.1399, pred[256]{0:T(512)(128)(4,1)S(1)} %compare_and_fusion.18, f32[128,8]{0,1:T(8,128)S(1)} %get-tuple-element.1227, ...), kind=kOutput, calls=%fused_computation.44.clone.1 | convolution fusion | flops 68157440 | bytes 2171648 | tf_op jit(solution)/shard_map/while/body/eval_jaxpr/rgk,kd->rgd/dot_general | solution.py:38
  60.9 1.7 %collective-permute-start.9 = (bf16[512,128]{1,0:T(8,128)(2,1)}, bf16[512,128]{1,0:T(8,128)(2,1)}, u32[]{:S(2)}, u32[]{:S(2)}) collective-permute-start(bf16[512,128]{1,0:T(8,128)(2,1)} %collective-permute-done.7), channel_id=1, source_target_pairs={{0,8},{8,16},{16,24},{24,32},{32,40},{40,48},{48,56},{56,64},{64,7... | collective-permute-start | bytes 393224 | tf_op jit(solution)/shard_map/ppermute | solution.py:15
  62.6 9.7 %while.116 = (s32[]{:T(128)}, f32[128,8,128]{2,0,1:T(8,128)S(1)}, f32[128,8]{0,1:T(8,128)S(1)}, f32[128,8]{0,1:T(8,128)S(1)}, s32[2]{0:T(128)S(1)}, /*index=5*/s...) while((s32[]{:T(128)}, f32[128,8,128]{2,0,1:T(8,128)S(1)}, ...), condition=%wide.region_26.27_spmd, body=%wide.region_23.26_spmd.sunk | while | flops 136842240 | bytes 4655225 | solution.py:58
  66.0 1.4 %convolution_add_fusion.20 = f32[128,8,128]{2,0,1:T(8,128)S(1)} fusion(f32[128,8,256]{0,2,1:T(8,128)S(1)} %get-tuple-element.1238, f32[128,8]{0,1:T(8,128)S(1)} %max.36, f32[128,8,128]{2,0,1:T(8,128)S(1)} %get-tuple-element.1429, pred[256]{0:T(512)(128)(4,1)S(1)} %compare_and_fusion.19, f32[128,8]{0,1:T(8,128)S(1)} %get-tuple-element.1240, ...), kind=kOutput, calls=%fused_computation.64.clone.1 | convolution fusion | flops 68157440 | bytes 2171648 | tf_op jit(solution)/shard_map/while/body/eval_jaxpr/rgk,kd->rgd/dot_general | solution.py:38
  68.1 1.4 %compare_and_fusion.19 = pred[256]{0:T(512)(128)(4,1)S(1)} fusion(s32[]{:T(128)} %get-tuple-element.1443, s32[]{:T(128)} %bitcast.208), kind=kLoop, calls=%fused_computation.77.clone.1 | loop fusion | flops 1024 | bytes 264 | tf_op jit(solution)/shard_map/while/body/eval_jaxpr/and | solution.py:55
  70.9 1.4 %convolution_add_fusion.20 = f32[128,8,128]{2,0,1:T(8,128)S(1)} fusion(f32[128,8,256]{0,2,1:T(8,128)S(1)} %get-tuple-element.1238, f32[128,8]{0,1:T(8,128)S(1)} %max.36, f32[128,8,128]{2,0,1:T(8,128)S(1)} %get-tuple-element.1429, pred[256]{0:T(512)(128)(4,1)S(1)} %compare_and_fusion.19, f32[128,8]{0,1:T(8,128)S(1)} %get-tuple-element.1240, ...), kind=kOutput, calls=%fused_computation.64.clone.1 | convolution fusion | flops 68157440 | bytes 2171648 | tf_op jit(solution)/shard_map/while/body/eval_jaxpr/rgk,kd->rgd/dot_general | solution.py:38
  72.5 3.2 %collective-permute-start.11 = (bf16[512,128]{1,0:T(8,128)(2,1)}, bf16[512,128]{1,0:T(8,128)(2,1)}, u32[]{:S(2)}, u32[]{:S(2)}) collective-permute-start(bf16[512,128]{1,0:T(8,128)(2,1)} %collective-permute-done.9), channel_id=1, source_target_pairs={{0,8},{8,16},{16,24},{24,32},{32,40},{40,48},{48,56},{56,64},{64,7... | collective-permute-start | bytes 393224 | tf_op jit(solution)/shard_map/ppermute | solution.py:15
  75.7 9.7 %while.117 = (s32[]{:T(128)}, f32[128,8,128]{2,0,1:T(8,128)S(1)}, f32[128,8]{0,1:T(8,128)S(1)}, f32[128,8]{0,1:T(8,128)S(1)}, s32[2]{0:T(128)S(1)}, /*index=5*/s...) while((s32[]{:T(128)}, f32[128,8,128]{2,0,1:T(8,128)S(1)}, ...), condition=%wide.region_31.32_spmd, body=%wide.region_28.31_spmd.sunk | while | flops 136842240 | bytes 4655225 | solution.py:58
  79.1 1.4 %convolution_add_fusion.21 = f32[128,8,128]{2,0,1:T(8,128)S(1)} fusion(f32[128,8,256]{0,2,1:T(8,128)S(1)} %get-tuple-element.1251, f32[128,8]{0,1:T(8,128)S(1)} %max.37, f32[128,8,128]{2,0,1:T(8,128)S(1)} %get-tuple-element.1459, pred[256]{0:T(512)(128)(4,1)S(1)} %compare_and_fusion.20, f32[128,8]{0,1:T(8,128)S(1)} %get-tuple-element.1253, ...), kind=kOutput, calls=%fused_computation.84.clone.1 | convolution fusion | flops 68157440 | bytes 2171648 | tf_op jit(solution)/shard_map/while/body/eval_jaxpr/rgk,kd->rgd/dot_general | solution.py:38
  84.0 1.4 %convolution_add_fusion.21 = f32[128,8,128]{2,0,1:T(8,128)S(1)} fusion(f32[128,8,256]{0,2,1:T(8,128)S(1)} %get-tuple-element.1251, f32[128,8]{0,1:T(8,128)S(1)} %max.37, f32[128,8,128]{2,0,1:T(8,128)S(1)} %get-tuple-element.1459, pred[256]{0:T(512)(128)(4,1)S(1)} %compare_and_fusion.20, f32[128,8]{0,1:T(8,128)S(1)} %get-tuple-element.1253, ...), kind=kOutput, calls=%fused_computation.84.clone.1 | convolution fusion | flops 68157440 | bytes 2171648 | tf_op jit(solution)/shard_map/while/body/eval_jaxpr/rgk,kd->rgd/dot_general | solution.py:38
  85.6 2.9 %collective-permute-start.13 = (bf16[512,128]{1,0:T(8,128)(2,1)}, bf16[512,128]{1,0:T(8,128)(2,1)S(1)}, u32[]{:S(2)}, u32[]{:S(2)}) collective-permute-start(bf16[512,128]{1,0:T(8,128)(2,1)} %collective-permute-done.11), channel_id=1, source_target_pairs={{0,8},{8,16},{16,24},{24,32},{32,40},{40,48},{48,56},{56,64},{64,7... | collective-permute-start | bytes 393224 | tf_op jit(solution)/shard_map/ppermute | solution.py:15
  88.5 9.6 %while.118 = (s32[]{:T(128)}, f32[128,8,128]{2,0,1:T(8,128)S(1)}, f32[128,8]{0,1:T(8,128)S(1)}, f32[128,8]{0,1:T(8,128)S(1)}, s32[2]{0:T(128)S(1)}, /*index=5*/s...) while((s32[]{:T(128)}, f32[128,8,128]{2,0,1:T(8,128)S(1)}, ...), condition=%wide.region_36.37_spmd, body=%wide.region_33.36_spmd.sunk | while | flops 136842240 | bytes 4655225 | solution.py:58
  91.8 1.4 %convolution_add_fusion.22 = f32[128,8,128]{2,0,1:T(8,128)S(1)} fusion(f32[128,8,256]{0,2,1:T(8,128)S(1)} %get-tuple-element.1264, f32[128,8]{0,1:T(8,128)S(1)} %max.38, f32[128,8,128]{2,0,1:T(8,128)S(1)} %get-tuple-element.1489, pred[256]{0:T(512)(128)(4,1)S(1)} %compare_and_fusion.21, f32[128,8]{0,1:T(8,128)S(1)} %get-tuple-element.1266, ...), kind=kOutput, calls=%fused_computation.104.clone.1 | convolution fusion | flops 68157440 | bytes 2171648 | tf_op jit(solution)/shard_map/while/body/eval_jaxpr/rgk,kd->rgd/dot_general | solution.py:38
  96.6 1.4 %convolution_add_fusion.22 = f32[128,8,128]{2,0,1:T(8,128)S(1)} fusion(f32[128,8,256]{0,2,1:T(8,128)S(1)} %get-tuple-element.1264, f32[128,8]{0,1:T(8,128)S(1)} %max.38, f32[128,8,128]{2,0,1:T(8,128)S(1)} %get-tuple-element.1489, pred[256]{0:T(512)(128)(4,1)S(1)} %compare_and_fusion.21, f32[128,8]{0,1:T(8,128)S(1)} %get-tuple-element.1266, ...), kind=kOutput, calls=%fused_computation.104.clone.1 | convolution fusion | flops 68157440 | bytes 2171648 | tf_op jit(solution)/shard_map/while/body/eval_jaxpr/rgk,kd->rgd/dot_general | solution.py:38
  98.1 6.2 %while.119 = (s32[]{:T(128)}, f32[128,8,128]{2,0,1:T(8,128)S(1)}, f32[128,8]{0,1:T(8,128)S(1)}, f32[128,8]{0,1:T(8,128)S(1)}, s32[2]{0:T(128)S(1)}, /*index=5*/s...) while((s32[]{:T(128)}, f32[128,8,128]{2,0,1:T(8,128)S(1)}, ...), condition=%wide.region_41.42_spmd, body=%wide.region_38.41_spmd.sunk | while | flops 136842240 | bytes 4654721 | solution.py:58
  104.8 13.0 %all_to_all.19 = bf16[8,16,1024]{2,1,0:T(8,128)(2,1)S(1)} all-to-all(bf16[8,16,1024]{2,1,0:T(8,128)(2,1)S(1)} %all_to_all.14), channel_id=1, replica_groups=mesh['ctx'=32,'kvh'=8] {'kvh'}, dimensions={0} | all-to-all | bytes 524288 | tf_op jit(solution)/shard_map/all_to_all | solution.py:106
  118.5 1.7 %fusion.158 = (bf16[4096,128]{1,0:T(8,128)(2,1)S(1)}, bf16[4096,128]{1,0:T(8,128)(2,1)S(1)}) fusion(bf16[4096,256]{1,0:T(8,128)(2,1)} %all-gather.2.cloned.1.call-done), kind=kLoop, calls=%fused_computation.222 | loop fusion | bytes 4194304 | tf_op jit(solution)/shard_map/split | solution.py:24
  (174 shorter events, 60.3 us)
Async XLA Ops:
  7.2 7.3 %copy-start = (bf16[512,128]{1,0:T(8,128)(2,1)S(1)}, bf16[512,128]{1,0:T(8,128)(2,1)}, u32[]{:S(2)}) copy-start(bf16[512,128]{1,0:T(8,128)(2,1)} %param.25) | copy-start | bytes 393220
  7.2 7.3 %copy-start.1 = (bf16[512,128]{1,0:T(8,128)(2,1)S(1)}, bf16[512,128]{1,0:T(8,128)(2,1)}, u32[]{:S(2)}) copy-start(bf16[512,128]{1,0:T(8,128)(2,1)} %param.26) | copy-start | bytes 393220
  7.2 6.0 %copy-start.2 = (bf16[128,128]{1,0:T(8,128)(2,1)S(1)}, bf16[128,128]{1,0:T(8,128)(2,1)}, u32[]{:S(2)}) copy-start(bf16[128,128]{1,0:T(8,128)(2,1)} %param.28) | copy-start | bytes 98308
  7.2 6.4 %copy-start.4 = (s32[32]{0:T(128)S(1)}, s32[32]{0:T(128)}, u32[]{:S(2)}) copy-start(s32[32]{0:T(128)} %param.29) | copy-start | bytes 388
  7.2 111.3 %all-gather.2.cloned.1.call-start = ((), (), s32[]{:S(2)}) async-start(), calls=%async_computation.1 | async-start | bytes 2162688 | tf_op jit(solution)/shard_map/all_gather | solution.py:24
  7.3 15.8 %collective-permute-start = (bf16[512,128]{1,0:T(8,128)(2,1)}, bf16[512,128]{1,0:T(8,128)(2,1)}, u32[]{:S(2)}, u32[]{:S(2)}) collective-permute-start(bf16[512,128]{1,0:T(8,128)(2,1)} %param.25), channel_id=1, source_target_pairs={{0,8},{8,16},{16,24},{24,32},{32,40},{40,48},{48,56},{56,64},{64,7... | collective-permute-start | bytes 393224 | tf_op jit(solution)/shard_map/ppermute | solution.py:15
  7.3 15.9 %collective-permute-start.1 = (bf16[512,128]{1,0:T(8,128)(2,1)}, bf16[512,128]{1,0:T(8,128)(2,1)}, u32[]{:S(2)}, u32[]{:S(2)}) collective-permute-start(bf16[512,128]{1,0:T(8,128)(2,1)} %param.26), channel_id=1, source_target_pairs={{0,8},{8,16},{16,24},{24,32},{32,40},{40,48},{48,56},{56,64},{64,7... | collective-permute-start | bytes 393224 | tf_op jit(solution)/shard_map/ppermute | solution.py:15
  23.0 12.8 %collective-permute-start.2 = (bf16[512,128]{1,0:T(8,128)(2,1)}, bf16[512,128]{1,0:T(8,128)(2,1)}, u32[]{:S(2)}, u32[]{:S(2)}) collective-permute-start(bf16[512,128]{1,0:T(8,128)(2,1)} %collective-permute-done), channel_id=1, source_target_pairs={{0,8},{8,16},{16,24},{24,32},{32,40},{40,48},{48,56},{56,64},{64,7... | collective-permute-start | bytes 393224 | tf_op jit(solution)/shard_map/ppermute | solution.py:15
  23.2 12.8 %collective-permute-start.3 = (bf16[512,128]{1,0:T(8,128)(2,1)}, bf16[512,128]{1,0:T(8,128)(2,1)}, u32[]{:S(2)}, u32[]{:S(2)}) collective-permute-start(bf16[512,128]{1,0:T(8,128)(2,1)} %collective-permute-done.1), channel_id=1, source_target_pairs={{0,8},{8,16},{16,24},{24,32},{32,40},{40,48},{48,56},{56,64},{64,7... | collective-permute-start | bytes 393224 | tf_op jit(solution)/shard_map/ppermute | solution.py:15
  35.8 11.5 %collective-permute-start.4 = (bf16[512,128]{1,0:T(8,128)(2,1)}, bf16[512,128]{1,0:T(8,128)(2,1)}, u32[]{:S(2)}, u32[]{:S(2)}) collective-permute-start(bf16[512,128]{1,0:T(8,128)(2,1)} %collective-permute-done.2), channel_id=1, source_target_pairs={{0,8},{8,16},{16,24},{24,32},{32,40},{40,48},{48,56},{56,64},{64,7... | collective-permute-start | bytes 393224 | tf_op jit(solution)/shard_map/ppermute | solution.py:15
  36.0 11.5 %collective-permute-start.5 = (bf16[512,128]{1,0:T(8,128)(2,1)}, bf16[512,128]{1,0:T(8,128)(2,1)}, u32[]{:S(2)}, u32[]{:S(2)}) collective-permute-start(bf16[512,128]{1,0:T(8,128)(2,1)} %collective-permute-done.3), channel_id=1, source_target_pairs={{0,8},{8,16},{16,24},{24,32},{32,40},{40,48},{48,56},{56,64},{64,7... | collective-permute-start | bytes 393224 | tf_op jit(solution)/shard_map/ppermute | solution.py:15
  47.3 13.2 %collective-permute-start.6 = (bf16[512,128]{1,0:T(8,128)(2,1)}, bf16[512,128]{1,0:T(8,128)(2,1)}, u32[]{:S(2)}, u32[]{:S(2)}) collective-permute-start(bf16[512,128]{1,0:T(8,128)(2,1)} %collective-permute-done.4), channel_id=1, source_target_pairs={{0,8},{8,16},{16,24},{24,32},{32,40},{40,48},{48,56},{56,64},{64,7... | collective-permute-start | bytes 393224 | tf_op jit(solution)/shard_map/ppermute | solution.py:15
  47.5 13.4 %collective-permute-start.7 = (bf16[512,128]{1,0:T(8,128)(2,1)}, bf16[512,128]{1,0:T(8,128)(2,1)}, u32[]{:S(2)}, u32[]{:S(2)}) collective-permute-start(bf16[512,128]{1,0:T(8,128)(2,1)} %collective-permute-done.5), channel_id=1, source_target_pairs={{0,8},{8,16},{16,24},{24,32},{32,40},{40,48},{48,56},{56,64},{64,7... | collective-permute-start | bytes 393224 | tf_op jit(solution)/shard_map/ppermute | solution.py:15
  60.5 11.8 %collective-permute-start.8 = (bf16[512,128]{1,0:T(8,128)(2,1)}, bf16[512,128]{1,0:T(8,128)(2,1)}, u32[]{:S(2)}, u32[]{:S(2)}) collective-permute-start(bf16[512,128]{1,0:T(8,128)(2,1)} %collective-permute-done.6), channel_id=1, source_target_pairs={{0,8},{8,16},{16,24},{24,32},{32,40},{40,48},{48,56},{56,64},{64,7... | collective-permute-start | bytes 393224 | tf_op jit(solution)/shard_map/ppermute | solution.py:15
  60.9 11.6 %collective-permute-start.9 = (bf16[512,128]{1,0:T(8,128)(2,1)}, bf16[512,128]{1,0:T(8,128)(2,1)}, u32[]{:S(2)}, u32[]{:S(2)}) collective-permute-start(bf16[512,128]{1,0:T(8,128)(2,1)} %collective-permute-done.7), channel_id=1, source_target_pairs={{0,8},{8,16},{16,24},{24,32},{32,40},{40,48},{48,56},{56,64},{64,7... | collective-permute-start | bytes 393224 | tf_op jit(solution)/shard_map/ppermute | solution.py:15
  72.3 13.1 %collective-permute-start.10 = (bf16[512,128]{1,0:T(8,128)(2,1)}, bf16[512,128]{1,0:T(8,128)(2,1)}, u32[]{:S(2)}, u32[]{:S(2)}) collective-permute-start(bf16[512,128]{1,0:T(8,128)(2,1)} %collective-permute-done.8), channel_id=1, source_target_pairs={{0,8},{8,16},{16,24},{24,32},{32,40},{40,48},{48,56},{56,64},{64,7... | collective-permute-start | bytes 393224 | tf_op jit(solution)/shard_map/ppermute | solution.py:15
  72.5 13.1 %collective-permute-start.11 = (bf16[512,128]{1,0:T(8,128)(2,1)}, bf16[512,128]{1,0:T(8,128)(2,1)}, u32[]{:S(2)}, u32[]{:S(2)}) collective-permute-start(bf16[512,128]{1,0:T(8,128)(2,1)} %collective-permute-done.9), channel_id=1, source_target_pairs={{0,8},{8,16},{16,24},{24,32},{32,40},{40,48},{48,56},{56,64},{64,7... | collective-permute-start | bytes 393224 | tf_op jit(solution)/shard_map/ppermute | solution.py:15
  85.4 12.6 %collective-permute-start.12 = (bf16[512,128]{1,0:T(8,128)(2,1)}, bf16[512,128]{1,0:T(8,128)(2,1)S(1)}, u32[]{:S(2)}, u32[]{:S(2)}) collective-permute-start(bf16[512,128]{1,0:T(8,128)(2,1)} %collective-permute-done.10), channel_id=1, source_target_pairs={{0,8},{8,16},{16,24},{24,32},{32,40},{40,48},{48,56},{56,64},{64,7... | collective-permute-start | bytes 393224 | tf_op jit(solution)/shard_map/ppermute | solution.py:15
  85.6 12.5 %collective-permute-start.13 = (bf16[512,128]{1,0:T(8,128)(2,1)}, bf16[512,128]{1,0:T(8,128)(2,1)S(1)}, u32[]{:S(2)}, u32[]{:S(2)}) collective-permute-start(bf16[512,128]{1,0:T(8,128)(2,1)} %collective-permute-done.11), channel_id=1, source_target_pairs={{0,8},{8,16},{16,24},{24,32},{32,40},{40,48},{48,56},{56,64},{64,7... | collective-permute-start | bytes 393224 | tf_op jit(solution)/shard_map/ppermute | solution.py:15
  120.2 1.0 copy-start.3
Sparse Core Ops, SparseCore 0:
  10.8 82.7 all-gather.1
where the time goes:
time: 131 us; the launch traced here: 129 us
  matrix products  35.9 us (27%)
  other arithmetic  30.7 us (23%)
  starting transfers between devices  19.1 us (15%)
  local copies, waits for them, and re-layouts  14.9 us (11%)
  between operations  14.5 us (11%)
  blocking collectives  13 us (10%)
    dot_general x17, matrix products, absorb(): jnp.einsum('rgk,kd->rgd', packed, value_rows, preferred_element_type=jnp....  19.3 us
    ppermute x14, starting transfers between devices, passed_along(): lax.ppermute(array, axis, [(i, (i + by) % size) for i in range(size)])  19.1 us
    and x16, other arithmetic, one_block(): (positions[None, :] < live_count) & (positions[None, :] <= limit_rows[:,...  18.9 us
    dot_general x17, matrix products, absorb(): jnp.einsum('rgd,kd->rgk', query, key_rows, preferred_element_type=jnp.flo...  16.1 us
    all_to_all x1, blocking collectives, per_device(): lax.all_to_all(result, 'kvh', split_axis=0, concat_axis=1, tiled=True)  13 us
    dynamic_slice x16, local copies, waits for them, and re-layouts, absorb_shard(): lax.scan(one_block, carry_state, (key_blocks, value_blocks, block_starts))  9.9 us
    reduce_sum x17, other arithmetic, absorb(): denominator = denominator * factor + jnp.sum(weights, axis=2)  3.5 us
  transfers between devices with their start and end apart: 15, of which 0 were waited for; matrix products, arithmetic and copies ran while one was open for 60% of the time, Pallas kernels for 0%

commit v1 on v0

v1 whole, which is shorter than its diff:
```python
import functools
import math

import jax
import jax.numpy as jnp
from jax import lax
from jax.experimental import pallas as pl
from jax.experimental.pallas import tpu as pltpu
from jax.sharding import PartitionSpec as P

MESH = pl.DeviceIdType.MESH
SPAN = 128
HD = 128
GROUP = 8
SHARD = 512
HALF = 256
LANES = 256
VROWS = 144
BF = jnp.bfloat16
F32 = jnp.float32

FIRST = (
    ((1, 0, 0, 1, 0, 1, 0), (1, 1, 0, 0, 0, 1, 0), (1, 0, 0, 0, 0, 0, 2), (1, 1, 0, 1, 0, 0, 2), (1, 0, 0, 1, 0, 0, 1), (1, 1, 0, 0, 0, 0, 1), (1, 0, 0, 0, 0, 1, 0), (1, 1, 0, 1, 0, 0, 1), (1, 0, 0, 1, 0, 0, 2), (1, 0, 0, 0, 0, 0, 1), (1, 1, 0, 0, 0, 0, 2)),
    ((1, 0, 1, 0, 0, 0, 3), (1, 0, 1, 1, 0, 1, 1), (1, 1, 1, 1, 0, 0, 3), (1, 1, 1, 0, 0, 0, 3), (1, 1, 1, 0, 0, 1, 1), (1, 0, 1, 1, 0, 0, 3), (1, 1, 1, 1, 0, 1, 1)),
    ((1, 1, 2, 1, 0, 1, 2), (1, 0, 2, 1, 0, 0, 3), (1, 1, 2, 1, 0, 0, 3), (1, 1, 2, 0, 0, 0, 3), (1, 0, 2, 0, 0, 1, 2), (1, 0, 2, 1, 0, 1, 2), (1, 0, 2, 0, 0, 0, 3), (1, 1, 2, 0, 0, 1, 2)),
    ((1, 0, 3, 1, 0, 1, 3), (1, 1, 3, 0, 0, 0, 1), (1, 0, 3, 0, 0, 1, 3), (1, 1, 3, 1, 0, 0, 1)),
)
SEQ = (
    (
        ((0, 0, 0, 1, 1), (1, 0, 0, 1, 1, 0, 1), (0, 1, 0, 0, 1), (1, 1, 0, 0, 1, 0, 1), (0, 0, 1, 1, 1), (0, 0, 0, 0, 1), (1, 0, 0, 0, 1, 0, 2), (1, 0, 0, 0, 1, 0, 1), (0, 1, 1, 0, 1), (0, 1, 2, 1, 1), (1, 1, 2, 1, 1, 1, 0), (1, 1, 2, 1, 1, 0, 1), (0, 1, 1, 1, 1), (0, 1, 1, 0, 2), (0, 1, 3, 0, 1), (0, 0, 2, 0, 1), (1, 0, 2, 0, 1, 0, 1), (1, 0, 2, 0, 1, 1, 0), (0, 1, 3, 1, 1), (0, 0, 3, 1, 1), (0, 1, 1, 1, 2), (0, 0, 2, 1, 1), (1, 0, 2, 1, 1, 0, 1), (1, 0, 2, 1, 1, 1, 0), (0, 0, 3, 0, 1)),
        ((0, 1, 2, 0, 1), (1, 1, 2, 0, 1, 0, 1)),
        ((0, 1, 2, 1, 2), (1, 1, 2, 1, 2, 0, 1), (0, 1, 3, 0, 2), (0, 1, 0, 1, 1), (1, 1, 0, 1, 1, 0, 1)),
        ((0, 0, 3, 1, 2), (0, 1, 3, 1, 2), (0, 0, 2, 0, 2), (1, 0, 2, 0, 2, 0, 1), (0, 1, 2, 0, 2), (1, 1, 2, 0, 2, 0, 1), (0, 0, 1, 0, 1)),
        ((0, 0, 2, 1, 2), (1, 0, 2, 1, 2, 0, 1)),
        ((0, 0, 3, 0, 2),),
        ((0, 0, 1, 0, 2), (0, 0, 1, 1, 2)),
    ),
    (
        ((0, 0, 0, 1, 0), (0, 1, 0, 0, 0), (0, 1, 0, 1, 0), (0, 0, 0, 0, 0)),
        ((0, 1, 3, 0, 0), (1, 1, 3, 0, 0, 1, 1), (0, 0, 1, 1, 1), (1, 0, 1, 1, 1, 0, 3), (1, 0, 1, 1, 1, 0, 0), (0, 1, 3, 1, 0), (1, 1, 3, 1, 0, 1, 1), (0, 1, 1, 0, 1), (1, 1, 1, 0, 1, 1, 0), (1, 1, 1, 0, 1, 0, 3), (1, 1, 1, 0, 1, 0, 0), (0, 0, 0, 1, 1), (0, 1, 1, 1, 1), (1, 1, 1, 1, 1, 0, 0), (1, 1, 1, 1, 1, 1, 0), (1, 1, 1, 1, 1, 0, 3), (0, 1, 0, 0, 1), (0, 1, 3, 0, 1), (1, 1, 3, 0, 1, 0, 3), (1, 1, 3, 0, 1, 1, 1), (1, 1, 3, 0, 1, 0, 0), (0, 1, 3, 1, 1), (1, 1, 3, 1, 1, 1, 1), (1, 1, 3, 1, 1, 0, 3), (1, 1, 3, 1, 1, 0, 0), (0, 0, 3, 1, 1), (1, 0, 3, 1, 1, 0, 0), (0, 0, 0, 0, 1), (0, 0, 3, 0, 1), (1, 0, 3, 0, 1, 1, 1), (1, 0, 3, 0, 1, 0, 0)),
        ((0, 1, 2, 1, 1), (0, 1, 3, 0, 2), (1, 1, 3, 0, 2, 0, 0), (0, 0, 2, 0, 1), (0, 0, 3, 1, 2), (1, 0, 3, 1, 2, 0, 0), (0, 0, 2, 1, 1), (0, 1, 3, 1, 2), (1, 1, 3, 1, 2, 0, 0), (1, 1, 3, 1, 2, 0, 2), (0, 0, 1, 0, 1), (1, 0, 1, 0, 1, 0, 0), (1, 0, 1, 0, 1, 1, 0)),
        ((0, 1, 2, 0, 1),),
        ((0, 0, 3, 0, 2), (1, 0, 3, 0, 2, 0, 0)),
        ((0, 1, 2, 1, 2), (0, 1, 0, 1, 1)),
        ((0, 0, 2, 0, 2), (0, 1, 2, 0, 2), (0, 0, 2, 1, 2)),
    ),
    (
        ((0, 1, 2, 1, 1), (1, 1, 2, 1, 1, 0, 0), (1, 1, 2, 1, 1, 0, 3), (0, 0, 0, 0, 0), (1, 0, 0, 0, 0, 0, 3), (0, 0, 2, 0, 1), (1, 0, 2, 0, 1, 0, 0), (1, 0, 2, 0, 1, 0, 3), (0, 0, 3, 1, 1), (0, 1, 0, 1, 0), (1, 1, 0, 1, 0, 1, 2), (1, 1, 0, 1, 0, 0, 3), (0, 0, 1, 0, 0), (0, 0, 2, 1, 1), (1, 0, 2, 1, 1, 0, 3), (1, 0, 2, 1, 1, 0, 0), (0, 0, 3, 0, 1), (0, 1, 2, 0, 1), (1, 1, 2, 0, 1, 0, 0), (1, 1, 2, 0, 1, 1, 2), (1, 1, 2, 0, 1, 0, 3)),
        ((0, 0, 0, 1, 0), (1, 0, 0, 1, 0, 1, 2), (1, 0, 0, 1, 0, 0, 3), (0, 1, 1, 1, 0), (0, 1, 0, 0, 0), (1, 1, 0, 0, 0, 1, 2), (1, 1, 0, 0, 0, 0, 3)),
        ((0, 1, 1, 0, 0), (0, 0, 3, 1, 2), (0, 0, 3, 0, 2), (0, 1, 0, 1, 1), (1, 1, 0, 1, 1, 0, 3), (1, 1, 0, 1, 1, 0, 0), (0, 0, 1, 0, 1), (0, 0, 1, 1, 0)),
        ((0, 1, 2, 0, 2), (1, 1, 2, 0, 2, 0, 0), (0, 0, 1, 1, 1), (0, 0, 0, 1, 1), (1, 0, 0, 1, 1, 0, 3), (0, 0, 0, 0, 1), (1, 0, 0, 0, 1, 0, 3), (0, 1, 0, 0, 1), (1, 1, 0, 0, 1, 0, 3)),
        ((0, 1, 1, 0, 1), (0, 1, 1, 1, 1)),
        ((0, 1, 3, 0, 1), (0, 1, 3, 1, 1)),
        ((0, 1, 3, 0, 2), (0, 1, 3, 1, 2)),
    ),
    (
        ((0, 0, 2, 1, 0), (0, 1, 2, 1, 0), (0, 1, 2, 0, 0), (0, 0, 2, 0, 0)),
        ((0, 0, 3, 1, 1), (1, 0, 3, 1, 1, 1, 3), (1, 0, 3, 1, 1, 0, 2), (1, 0, 3, 1, 1, 0, 1), (0, 0, 1, 0, 0), (1, 0, 1, 0, 0, 1, 3), (1, 0, 1, 0, 0, 0, 2), (0, 0, 3, 0, 1), (1, 0, 3, 0, 1, 0, 2), (1, 0, 3, 0, 1, 1, 2), (1, 0, 3, 0, 1, 0, 1), (0, 1, 2, 1, 1), (0, 1, 1, 1, 0), (1, 1, 1, 1, 0, 0, 2), (0, 0, 0, 0, 0), (0, 0, 2, 0, 1), (0, 1, 1, 0, 0), (1, 1, 1, 0, 0, 0, 2), (0, 1, 0, 1, 0), (0, 0, 3, 1, 2), (1, 0, 3, 1, 2, 0, 1), (1, 0, 3, 1, 2, 0, 2), (0, 0, 2, 1, 1), (0, 0, 1, 0, 1), (1, 0, 1, 0, 1, 0, 1), (1, 0, 1, 0, 1, 0, 2), (0, 0, 1, 1, 0), (1, 0, 1, 1, 0, 0, 2)),
        ((0, 1, 2, 0, 1),),
        ((0, 0, 0, 1, 0), (0, 0, 1, 1, 1), (1, 0, 1, 1, 1, 1, 3), (1, 0, 1, 1, 1, 0, 2), (0, 1, 0, 0, 0)),
        ((0, 1, 1, 0, 1), (1, 1, 1, 0, 1, 0, 2), (0, 1, 0, 1, 1), (0, 1, 1, 1, 1), (1, 1, 1, 1, 1, 0, 2)),
        ((0, 1, 3, 0, 1), (1, 1, 3, 0, 1, 1, 2), (1, 1, 3, 0, 1, 0, 2), (0, 0, 1, 1, 2), (1, 0, 1, 1, 2, 0, 0), (0, 0, 0, 1, 1), (0, 0, 0, 0, 1), (0, 1, 3, 1, 1), (1, 1, 3, 1, 1, 0, 2)),
        ((0, 1, 0, 0, 1),),
    ),
)
ORDER = ((7, 6, 4, 5, 10, 11, 9), (0, 7, 5, 6, 11, 4, 10), (6, 0, 1, 4, 5, 7, 11), (2, 1, 6, 0, 5, 7, 4))
SPREAD = (1, 2, 3)


def slot_of(age, home):
    return age * 4 + home


def per_device(
    queries, cache_keys, cache_values, new_keys, new_values, cache_fill, span_pos, destination
):
    n_ctx = lax.axis_size("ctx")
    n_kvh = lax.axis_size("kvh")
    planes = n_ctx // 4
    pieces = n_ctx
    scaling = HD ** (-0.5) * math.log2(math.e)

    def kernel(
        q_ref, ck_ref, cv_ref, nk_ref, nv_ref, fill_ref, pos_ref, dest_ref,
        out_ref, ak_ref, av_ref,
        qt_ref, kb, vb, nvt, acc, m_ref, obuf, arecv, pk, w1, w2, app,
        ss, rs, a_s, a_r, w1s, w1r, w2s, w2r, spread,
    ):
        me = lax.axis_index("ctx")
        head = lax.axis_index("kvh")
        plane = me // 4
        role = lax.rem(me, 4)

        def at(up, r):
            return (lax.rem(plane + up + planes, planes) * 4 + r, head)

        barrier = pltpu.get_barrier_semaphore()
        near = [at(0, role ^ 1), at(0, role ^ 2), at(0, role ^ 3)]
        near += [at(1, role), at(-1, role), at(1, role ^ 1), at(-1, role ^ 1)]
        near += [(me, lax.rem(head + i, n_kvh)) for i in range(1, n_kvh)]
        for device in near:
            pl.semaphore_signal(barrier, inc=1, device_id=device, device_id_type=MESH)

        own = role
        live = fill_ref[me]
        keys = ck_ref[...].astype(F32)
        alive = lax.broadcasted_iota(jnp.int32, (SHARD, HD), 0) < live
        keys = jnp.where(alive, keys, keys[0:1, :]).astype(BF)
        values = jnp.where(alive, cv_ref[...].astype(F32), 0.0)
        for c in range(2):
            kb[own, c] = keys[c * HALF:(c + 1) * HALF]
            vb[own, c, 0:HD, :] = values[c * HALF:(c + 1) * HALF].T.astype(BF)
        for i in range(pieces // 2):
            pk[i] = nk_ref[i]
            pk[i + pieces // 2] = nv_ref[i]

        pl.semaphore_wait(barrier, len(near))

        sends = {}

        def piece(t, j, c, age):
            if t == 0:
                return kb.at[slot_of(age, j), c]
            return vb.at[slot_of(age, j), c, pl.ds(0, HD)]

        def remote(t, j, c, age, up, r, index):
            return pltpu.make_async_remote_copy(
                src_ref=piece(t, j, c, age),
                dst_ref=piece(t, j, c, age + up),
                send_sem=ss.at[index],
                recv_sem=rs.at[t, slot_of(age + up, j), c],
                device_id=at(up, r),
                device_id_type=MESH,
            )

        def act(r, action):
            if action[0] == 0:
                _, t, j, c, age = action
                pltpu.make_async_remote_copy(
                    src_ref=piece(t, j, c, age),
                    dst_ref=piece(t, j, c, age),
                    send_sem=ss.at[0],
                    recv_sem=rs.at[t, slot_of(age, j), c],
                    device_id=at(0, role ^ 1),
                    device_id_type=MESH,
                ).wait_recv()
            else:
                done = sends.setdefault(r, [])
                remote(*action[1:], len(done)).start()
                done.append(action[1:])

        for r in range(4):
            @pl.when(role == r)
            def _(r=r):
                for action in FIRST[r]:
                    act(r, action)

        def signal_planes(k, step):
            for up in (step, -step):
                pl.semaphore_signal(spread.at[k], inc=1, device_id=at(up, role), device_id_type=MESH)

        signal_planes(0, 1)

        for b in range(SPAN // 16):
            rows = [q_ref[b * 16:(b + 1) * 16, g * HD:(g + 1) * HD] for g in range(GROUP)]
            block = jnp.concatenate(rows, axis=0)
            qt_ref[:, b * 128:(b + 1) * 128] = block.astype(F32).T.astype(BF)
        row16 = lax.broadcasted_iota(jnp.int32, (16, HALF), 0)
        lane16 = lax.broadcasted_iota(jnp.int32, (16, HALF), 1)
        nvt[0:HD, :] = nv_ref[...].reshape(SPAN, HD).astype(F32).T.astype(BF)
        nvt[HD:VROWS, :] = jnp.where(row16[:, :SPAN] == 0, 1.0, 0.0).astype(BF)
        for age in range(3):
            for j in range(4):
                filled = fill_ref[at(-age, j)[0]]
                for c in range(2):
                    seen = (row16 == 0) & (lane16 + c * HALF < filled)
                    vb[slot_of(age, j), c, HD:VROWS, :] = jnp.where(seen, 1.0, 0.0).astype(BF)

        def tokens(tile, rows):
            lane = lax.broadcasted_iota(jnp.int32, (rows, LANES), 1)
            return (tile * 2 + lane // 128) * 16 + lane % 16

        def dot(a, b):
            return jnp.dot(a, b, preferred_element_type=F32)

        def lanes_of(tile):
            if isinstance(tile, int):
                return pl.ds(tile * LANES, LANES)
            return pl.ds(pl.multiple_of(tile * LANES, LANES), LANES)

        tiles = (GROUP * SPAN) // LANES

        for tile in range(tiles):
            lanes = lanes_of(tile)
            s = dot(nk_ref[...].reshape(SPAN, HD), qt_ref[:, lanes])
            row = lax.broadcasted_iota(jnp.int32, (SPAN, LANES), 0)
            s = jnp.where(row <= tokens(tile, SPAN), s, -1e30)
            top = jnp.max(s, axis=0, keepdims=True)
            weights = jnp.exp2((s - top) * scaling).astype(BF)
            acc[:, lanes] = dot(nvt[...], weights)
            m_ref[:, lanes] = top

        def attend(tile, slot, home):
            lanes = lanes_of(tile)
            qt = qt_ref[:, lanes]
            parts = []
            for c in range(2):
                s = dot(kb[slot, c], qt)
                if home:
                    row = lax.broadcasted_iota(jnp.int32, (HALF, LANES), 0) + c * HALF
                    s = jnp.where(row <= tokens(tile, HALF) + pos_ref[0], s, -1e30)
                parts.append(s)
            old = m_ref[:, lanes]
            top = jnp.maximum(old, jnp.max(jnp.maximum(parts[0], parts[1]), axis=0, keepdims=True))
            total = acc[:, lanes] * jnp.exp2((old - top) * scaling)
            for c in range(2):
                weights = jnp.exp2((parts[c] - top) * scaling).astype(BF)
                total = total + dot(vb[slot, c], weights)
            acc[:, lanes] = total
            m_ref[:, lanes] = top

        for tile in range(tiles):
            attend(tile, own, True)

        def spread_round(k):
            pl.semaphore_wait(spread.at[k], 2)
            if k == 0:
                signal_planes(1, 2)
            elif k == 1:
                signal_planes(2, 1)

        def stage_copy(src, dst, sems, semr, device, k, source):
            return pltpu.make_async_remote_copy(
                src_ref=src, dst_ref=dst, send_sem=sems.at[k], recv_sem=semr.at[source],
                device_id=(device, head), device_id_type=MESH,
            )

        def other(k):
            return lax.rem(me + k, n_ctx)

        def stage_one():
            w1[me] = pk[me]

            @pl.loop(1, n_ctx)
            def _(k):
                stage_copy(pk.at[other(k)], w1.at[me], w1s, w1r, other(k), k, me).start()

        def stage_two():
            @pl.loop(1, n_ctx)
            def _(k):
                d = other(k)
                stage_copy(pk.at[d], w1.at[d], w1s, w1r, d, k, d).wait()

            @pl.loop(0, n_ctx)
            def _(d):
                source = jnp.int32(0)
                for g in range(n_ctx):
                    source = jnp.maximum(source, jnp.where(dest_ref[g] == d, g, 0))
                w2[d] = w1[source]

            app[me] = w2[me]

            @pl.loop(1, n_ctx)
            def _(k):
                stage_copy(w2.at[other(k)], app.at[me], w2s, w2r, other(k), k, me).start()

        def communicate(step):
            for r in range(4):
                @pl.when(role == r)
                def _(r=r):
                    for i in range(7):
                        if SEQ[r][i]:
                            @pl.when(step == i)
                            def _(i=i):
                                for action in SEQ[r][i]:
                                    act(r, action)
            for k in range(3):
                @pl.when(step == SPREAD[k])
                def _(k=k):
                    spread_round(k)

            @pl.when(step == SPREAD[2])
            def _():
                stage_one()

            @pl.when(step == 6)
            def _():
                stage_two()

        def slot_at(step):
            slot = jnp.int32(0)
            for r in range(4):
                code = jnp.int32(ORDER[r][0])
                for i in range(1, 7):
                    code = jnp.where(step == i, ORDER[r][i], code)
                slot = jnp.where(role == r, code, slot)
            return slot

        @pl.loop(0, 6)
        def _(step):
            communicate(step)
            slot = slot_at(step)
            for tile in range(tiles):
                attend(tile, slot, False)

        communicate(6)
        last = slot_at(6)

        def out_copy(b):
            return pltpu.make_async_remote_copy(
                src_ref=obuf.at[b], dst_ref=arecv.at[head], send_sem=a_s.at[b], recv_sem=a_r.at[head],
                device_id=(me, b), device_id_type=MESH,
            )

        def ship(tile):
            for half in range(2):
                b = tile * 2 + half

                @pl.when(b != head)
                def _():
                    out_copy(b).start()

                @pl.when(b == head)
                def _():
                    arecv[b] = obuf[b]

        previous = None
        for i in range(tiles):
            tile = lax.rem(head // 2 + 1 + i, tiles)
            attend(tile, last, False)
            lanes = lanes_of(tile)
            result = acc[0:HD, lanes] * (1.0 / acc[HD:HD + 1, lanes])
            result = result.T.astype(BF)
            for half in range(2):
                for g in range(GROUP):
                    at_row = half * 128 + g * 16
                    obuf[tile * 2 + half, :, g * HD:(g + 1) * HD] = result[at_row:at_row + 16]
            if previous is not None:
                ship(previous)
            previous = tile
        ship(previous)

        for k in range(1, n_kvh):
            h = lax.rem(head + k, n_kvh)
            pltpu.make_async_remote_copy(
                src_ref=obuf.at[h], dst_ref=arecv.at[h], send_sem=a_s.at[h], recv_sem=a_r.at[h],
                device_id=(me, h), device_id_type=MESH,
            ).wait()
        for h in range(n_kvh):
            out_ref[:, h * GROUP * HD:(h + 1) * GROUP * HD] = arecv[h]

        @pl.loop(1, n_ctx)
        def _(k):
            d = other(k)
            stage_copy(w2.at[d], app.at[d], w2s, w2r, d, k, d).wait()

        for i in range(pieces // 2):
            ak_ref[i] = app[i]
            av_ref[i] = app[i + pieces // 2]

        for r in range(4):
            @pl.when(role == r)
            def _(r=r):
                for index, what in enumerate(sends[r]):
                    remote(*what, index).wait_send()

    half = pieces // 2
    rows8 = SPAN // half
    vmem = pl.BlockSpec(memory_space=pltpu.VMEM)
    smem = pl.BlockSpec(memory_space=pltpu.SMEM)
    dma = pltpu.SemaphoreType.DMA
    attn, keys, values = pl.pallas_call(
        kernel,
        out_shape=(
            jax.ShapeDtypeStruct((SPAN // n_kvh, n_kvh * GROUP * HD), BF),
            jax.ShapeDtypeStruct((half, rows8, HD), BF),
            jax.ShapeDtypeStruct((half, rows8, HD), BF),
        ),
        in_specs=[vmem] * 5 + [smem] * 3,
        out_specs=(vmem, vmem, vmem),
        scratch_shapes=[
            pltpu.VMEM((HD, GROUP * SPAN), BF),
            pltpu.VMEM((12, 2, HALF, HD), BF),
            pltpu.VMEM((12, 2, VROWS, HALF), BF),
            pltpu.VMEM((VROWS, SPAN), BF),
            pltpu.VMEM((VROWS, GROUP * SPAN), F32),
            pltpu.VMEM((1, GROUP * SPAN), F32),
            pltpu.VMEM((n_kvh, SPAN // n_kvh, GROUP * HD), BF),
            pltpu.VMEM((n_kvh, SPAN // n_kvh, GROUP * HD), BF),
            pltpu.VMEM((pieces, rows8, HD), BF),
            pltpu.VMEM((pieces, rows8, HD), BF),
            pltpu.VMEM((pieces, rows8, HD), BF),
            pltpu.VMEM((pieces, rows8, HD), BF),
            dma((48,)),
            dma((2, 12, 2)),
            dma((n_kvh,)),
            dma((n_kvh,)),
            dma((n_ctx,)),
            dma((n_ctx,)),
            dma((n_ctx,)),
            dma((n_ctx,)),
            pltpu.SemaphoreType.REGULAR((3,)),
        ],
        compiler_params=pltpu.CompilerParams(collective_id=0, has_side_effects=True),
        name="spanned_attention",
    )(
        queries, cache_keys, cache_values,
        new_keys.reshape(half, rows8, HD), new_values.reshape(half, rows8, HD),
        cache_fill, span_pos, destination,
    )
    return attn, keys.reshape(SPAN, HD), values.reshape(SPAN, HD)


def solution(mesh):
    placed = (
        P("ctx", "kvh"),
        P("ctx", "kvh"),
        P("ctx", "kvh"),
        P("ctx", "kvh"),
        P("ctx", "kvh"),
        P(),
        P("ctx"),
        P(),
    )
    return jax.shard_map(
        per_device,
        mesh=mesh,
        in_specs=placed,
        out_specs=(P(("ctx", "kvh"), None), P("ctx", "kvh"), P("ctx", "kvh")),
        check_vma=False,
    )
```

time: 131 us -> 49 us (0.37)
  the two profiles are of different devices: /device:TPU:16 before, /device:TPU:1 now
where the time goes in v1:
time: 49 us; the launch traced here: 48.8 us
  Pallas kernels  44.4 us (91%)
  local copies, waits for them, and re-layouts  3.06 us (6%)
  between operations  1.3 us (3%)
    pallas_call x1, Pallas kernels, per_device(): pl.pallas_call(kernel, out_shape=(jax.ShapeDtypeStruct((SPAN // n_kvh, n_...  44.4 us
    unnamed x7, local copies, waits for them, and re-layouts  3.06 us

profile of v1, /device:TPU:1, one launch (start us, length us, event | category | flops | bytes accessed | tf_op | source)
XLA Modules:
  0.0 48.8 jit_solution(493823244639179877)
XLA Ops:
  1.3 44.4 %spanned_attention.1 = (bf16[16,8192]{1,0:T(8,128)(2,1)}, bf16[16,8,128]{2,1,0:T(8,128)(2,1)}, bf16[16,8,128]{2,1,0:T(8,128)(2,1)}) custom-call(bf16[128,1024]{1,0:T(8,128)(2,1)} %q_ref.1, bf16[512,128]{1,0:T(8,128)(2,1)} %ck_ref.1, bf16[512,128]{1,0:T(8,128)(2,1)} %cv_ref.1, bf16[16,8,128]{2,1,0:T(8,128)(2,1)} %bitcast.6, bf16[16,8,128]{2,1,0:T(8,128)(2,1)} %bitcast.7, ...), custom_call_target="tpu_custom_call" | custom-call | tf_op jit(solution)/shard_map/spanned_attention/pallas_call | solution.py:372
  45.7 0.0 copy-start.1
  45.7 1.7 %copy.15 = bf16[16,8192]{1,0:T(8,128)(2,1)} copy(bf16[16,8192]{1,0:T(8,128)(2,1)} %get-tuple-element.12) | data formatting | bytes 524288
  47.4 0.0 copy-done.1
  47.4 0.0 copy-start
  47.4 0.6 %copy.16 = bf16[128,128]{1,0:T(8,128)(2,1)} copy(bf16[128,128]{1,0:T(8,128)(2,1)S(1)} %bitcast.5) | data formatting | bytes 65536
  48.0 0.2 copy-done
  48.2 0.6 %copy.17 = bf16[128,128]{1,0:T(8,128)(2,1)} copy(bf16[128,128]{1,0:T(8,128)(2,1)S(1)} %bitcast.4) | data formatting | bytes 65536
Async XLA Ops:
  45.7 1.7 %copy-start.1 = (bf16[16,8,128]{2,1,0:T(8,128)(2,1)S(1)}, bf16[16,8,128]{2,1,0:T(8,128)(2,1)}, u32[]{:S(2)}) copy-start(bf16[16,8,128]{2,1,0:T(8,128)(2,1)} %get-tuple-element.7) | copy-start | bytes 98308
  47.4 0.8 %copy-start = (bf16[16,8,128]{2,1,0:T(8,128)(2,1)S(1)}, bf16[16,8,128]{2,1,0:T(8,128)(2,1)}, u32[]{:S(2)}) copy-start(bf16[16,8,128]{2,1,0:T(8,128)(2,1)} %get-tuple-element.8) | copy-start | bytes 98308

commit v2 on v1

--- a/solution.py
+++ b/solution.py
@@ -16,6 +16,7 @@
 HALF = 256
 LANES = 256
 VROWS = 144
+AHEAD = 4
 BF = jnp.bfloat16
 F32 = jnp.float32
 
@@ -27,7 +28,7 @@
 )
 SEQ = (
     (
-        ((0, 0, 0, 1, 1), (1, 0, 0, 1, 1, 0, 1), (0, 1, 0, 0, 1), (1, 1, 0, 0, 1, 0, 1), (0, 0, 1, 1, 1), (0, 0, 0, 0, 1), (1, 0, 0, 0, 1, 0, 2), (1, 0, 0, 0, 1, 0, 1), (0, 1, 1, 0, 1), (0, 1, 2, 1, 1), (1, 1, 2, 1, 1, 1, 0), (1, 1, 2, 1, 1, 0, 1), (0, 1, 1, 1, 1), (0, 1, 1, 0, 2), (0, 1, 3, 0, 1), (0, 0, 2, 0, 1), (1, 0, 2, 0, 1, 0, 1), (1, 0, 2, 0, 1, 1, 0), (0, 1, 3, 1, 1), (0, 0, 3, 1, 1), (0, 1, 1, 1, 2), (0, 0, 2, 1, 1), (1, 0, 2, 1, 1, 0, 1), (1, 0, 2, 1, 1, 1, 0), (0, 0, 3, 0, 1)),
+        ((2, 0), (0, 0, 0, 1, 1), (1, 0, 0, 1, 1, 0, 1), (0, 1, 0, 0, 1), (1, 1, 0, 0, 1, 0, 1), (0, 0, 1, 1, 1), (2, 1), (0, 0, 0, 0, 1), (1, 0, 0, 0, 1, 0, 2), (1, 0, 0, 0, 1, 0, 1), (0, 1, 1, 0, 1), (0, 1, 2, 1, 1), (1, 1, 2, 1, 1, 1, 0), (1, 1, 2, 1, 1, 0, 1), (0, 1, 1, 1, 1), (0, 1, 1, 0, 2), (0, 1, 3, 0, 1), (2, 2), (3,), (0, 0, 2, 0, 1), (1, 0, 2, 0, 1, 0, 1), (1, 0, 2, 0, 1, 1, 0), (0, 1, 3, 1, 1), (0, 0, 3, 1, 1), (0, 1, 1, 1, 2), (0, 0, 2, 1, 1), (1, 0, 2, 1, 1, 0, 1), (1, 0, 2, 1, 1, 1, 0), (0, 0, 3, 0, 1)),
         ((0, 1, 2, 0, 1), (1, 1, 2, 0, 1, 0, 1)),
         ((0, 1, 2, 1, 2), (1, 1, 2, 1, 2, 0, 1), (0, 1, 3, 0, 2), (0, 1, 0, 1, 1), (1, 1, 0, 1, 1, 0, 1)),
         ((0, 0, 3, 1, 2), (0, 1, 3, 1, 2), (0, 0, 2, 0, 2), (1, 0, 2, 0, 2, 0, 1), (0, 1, 2, 0, 2), (1, 1, 2, 0, 2, 0, 1), (0, 0, 1, 0, 1)),
@@ -37,7 +38,7 @@
     ),
     (
         ((0, 0, 0, 1, 0), (0, 1, 0, 0, 0), (0, 1, 0, 1, 0), (0, 0, 0, 0, 0)),
-        ((0, 1, 3, 0, 0), (1, 1, 3, 0, 0, 1, 1), (0, 0, 1, 1, 1), (1, 0, 1, 1, 1, 0, 3), (1, 0, 1, 1, 1, 0, 0), (0, 1, 3, 1, 0), (1, 1, 3, 1, 0, 1, 1), (0, 1, 1, 0, 1), (1, 1, 1, 0, 1, 1, 0), (1, 1, 1, 0, 1, 0, 3), (1, 1, 1, 0, 1, 0, 0), (0, 0, 0, 1, 1), (0, 1, 1, 1, 1), (1, 1, 1, 1, 1, 0, 0), (1, 1, 1, 1, 1, 1, 0), (1, 1, 1, 1, 1, 0, 3), (0, 1, 0, 0, 1), (0, 1, 3, 0, 1), (1, 1, 3, 0, 1, 0, 3), (1, 1, 3, 0, 1, 1, 1), (1, 1, 3, 0, 1, 0, 0), (0, 1, 3, 1, 1), (1, 1, 3, 1, 1, 1, 1), (1, 1, 3, 1, 1, 0, 3), (1, 1, 3, 1, 1, 0, 0), (0, 0, 3, 1, 1), (1, 0, 3, 1, 1, 0, 0), (0, 0, 0, 0, 1), (0, 0, 3, 0, 1), (1, 0, 3, 0, 1, 1, 1), (1, 0, 3, 0, 1, 0, 0)),
+        ((2, 0), (0, 1, 3, 0, 0), (1, 1, 3, 0, 0, 1, 1), (0, 0, 1, 1, 1), (1, 0, 1, 1, 1, 0, 3), (1, 0, 1, 1, 1, 0, 0), (0, 1, 3, 1, 0), (1, 1, 3, 1, 0, 1, 1), (0, 1, 1, 0, 1), (1, 1, 1, 0, 1, 1, 0), (1, 1, 1, 0, 1, 0, 3), (1, 1, 1, 0, 1, 0, 0), (0, 0, 0, 1, 1), (2, 1), (0, 1, 1, 1, 1), (1, 1, 1, 1, 1, 0, 0), (1, 1, 1, 1, 1, 1, 0), (1, 1, 1, 1, 1, 0, 3), (0, 1, 0, 0, 1), (0, 1, 3, 0, 1), (1, 1, 3, 0, 1, 0, 3), (1, 1, 3, 0, 1, 1, 1), (1, 1, 3, 0, 1, 0, 0), (0, 1, 3, 1, 1), (1, 1, 3, 1, 1, 1, 1), (1, 1, 3, 1, 1, 0, 3), (1, 1, 3, 1, 1, 0, 0), (0, 0, 3, 1, 1), (1, 0, 3, 1, 1, 0, 0), (0, 0, 0, 0, 1), (2, 2), (3,), (0, 0, 3, 0, 1), (1, 0, 3, 0, 1, 1, 1), (1, 0, 3, 0, 1, 0, 0)),
         ((0, 1, 2, 1, 1), (0, 1, 3, 0, 2), (1, 1, 3, 0, 2, 0, 0), (0, 0, 2, 0, 1), (0, 0, 3, 1, 2), (1, 0, 3, 1, 2, 0, 0), (0, 0, 2, 1, 1), (0, 1, 3, 1, 2), (1, 1, 3, 1, 2, 0, 0), (1, 1, 3, 1, 2, 0, 2), (0, 0, 1, 0, 1), (1, 0, 1, 0, 1, 0, 0), (1, 0, 1, 0, 1, 1, 0)),
         ((0, 1, 2, 0, 1),),
         ((0, 0, 3, 0, 2), (1, 0, 3, 0, 2, 0, 0)),
@@ -45,9 +46,9 @@
         ((0, 0, 2, 0, 2), (0, 1, 2, 0, 2), (0, 0, 2, 1, 2)),
     ),
     (
-        ((0, 1, 2, 1, 1), (1, 1, 2, 1, 1, 0, 0), (1, 1, 2, 1, 1, 0, 3), (0, 0, 0, 0, 0), (1, 0, 0, 0, 0, 0, 3), (0, 0, 2, 0, 1), (1, 0, 2, 0, 1, 0, 0), (1, 0, 2, 0, 1, 0, 3), (0, 0, 3, 1, 1), (0, 1, 0, 1, 0), (1, 1, 0, 1, 0, 1, 2), (1, 1, 0, 1, 0, 0, 3), (0, 0, 1, 0, 0), (0, 0, 2, 1, 1), (1, 0, 2, 1, 1, 0, 3), (1, 0, 2, 1, 1, 0, 0), (0, 0, 3, 0, 1), (0, 1, 2, 0, 1), (1, 1, 2, 0, 1, 0, 0), (1, 1, 2, 0, 1, 1, 2), (1, 1, 2, 0, 1, 0, 3)),
+        ((2, 0), (0, 1, 2, 1, 1), (1, 1, 2, 1, 1, 0, 0), (1, 1, 2, 1, 1, 0, 3), (0, 0, 0, 0, 0), (1, 0, 0, 0, 0, 0, 3), (0, 0, 2, 0, 1), (1, 0, 2, 0, 1, 0, 0), (1, 0, 2, 0, 1, 0, 3), (0, 0, 3, 1, 1), (0, 1, 0, 1, 0), (1, 1, 0, 1, 0, 1, 2), (1, 1, 0, 1, 0, 0, 3), (0, 0, 1, 0, 0), (0, 0, 2, 1, 1), (1, 0, 2, 1, 1, 0, 3), (1, 0, 2, 1, 1, 0, 0), (2, 1), (0, 0, 3, 0, 1), (0, 1, 2, 0, 1), (1, 1, 2, 0, 1, 0, 0), (1, 1, 2, 0, 1, 1, 2), (1, 1, 2, 0, 1, 0, 3)),
         ((0, 0, 0, 1, 0), (1, 0, 0, 1, 0, 1, 2), (1, 0, 0, 1, 0, 0, 3), (0, 1, 1, 1, 0), (0, 1, 0, 0, 0), (1, 1, 0, 0, 0, 1, 2), (1, 1, 0, 0, 0, 0, 3)),
-        ((0, 1, 1, 0, 0), (0, 0, 3, 1, 2), (0, 0, 3, 0, 2), (0, 1, 0, 1, 1), (1, 1, 0, 1, 1, 0, 3), (1, 1, 0, 1, 1, 0, 0), (0, 0, 1, 0, 1), (0, 0, 1, 1, 0)),
+        ((0, 1, 1, 0, 0), (0, 0, 3, 1, 2), (2, 2), (3,), (0, 0, 3, 0, 2), (0, 1, 0, 1, 1), (1, 1, 0, 1, 1, 0, 3), (1, 1, 0, 1, 1, 0, 0), (0, 0, 1, 0, 1), (0, 0, 1, 1, 0)),
         ((0, 1, 2, 0, 2), (1, 1, 2, 0, 2, 0, 0), (0, 0, 1, 1, 1), (0, 0, 0, 1, 1), (1, 0, 0, 1, 1, 0, 3), (0, 0, 0, 0, 1), (1, 0, 0, 0, 1, 0, 3), (0, 1, 0, 0, 1), (1, 1, 0, 0, 1, 0, 3)),
         ((0, 1, 1, 0, 1), (0, 1, 1, 1, 1)),
         ((0, 1, 3, 0, 1), (0, 1, 3, 1, 1)),
@@ -55,16 +56,16 @@
     ),
     (
         ((0, 0, 2, 1, 0), (0, 1, 2, 1, 0), (0, 1, 2, 0, 0), (0, 0, 2, 0, 0)),
-        ((0, 0, 3, 1, 1), (1, 0, 3, 1, 1, 1, 3), (1, 0, 3, 1, 1, 0, 2), (1, 0, 3, 1, 1, 0, 1), (0, 0, 1, 0, 0), (1, 0, 1, 0, 0, 1, 3), (1, 0, 1, 0, 0, 0, 2), (0, 0, 3, 0, 1), (1, 0, 3, 0, 1, 0, 2), (1, 0, 3, 0, 1, 1, 2), (1, 0, 3, 0, 1, 0, 1), (0, 1, 2, 1, 1), (0, 1, 1, 1, 0), (1, 1, 1, 1, 0, 0, 2), (0, 0, 0, 0, 0), (0, 0, 2, 0, 1), (0, 1, 1, 0, 0), (1, 1, 1, 0, 0, 0, 2), (0, 1, 0, 1, 0), (0, 0, 3, 1, 2), (1, 0, 3, 1, 2, 0, 1), (1, 0, 3, 1, 2, 0, 2), (0, 0, 2, 1, 1), (0, 0, 1, 0, 1), (1, 0, 1, 0, 1, 0, 1), (1, 0, 1, 0, 1, 0, 2), (0, 0, 1, 1, 0), (1, 0, 1, 1, 0, 0, 2)),
+        ((2, 0), (0, 0, 3, 1, 1), (1, 0, 3, 1, 1, 1, 3), (1, 0, 3, 1, 1, 0, 2), (1, 0, 3, 1, 1, 0, 1), (0, 0, 1, 0, 0), (1, 0, 1, 0, 0, 1, 3), (1, 0, 1, 0, 0, 0, 2), (0, 0, 3, 0, 1), (1, 0, 3, 0, 1, 0, 2), (1, 0, 3, 0, 1, 1, 2), (1, 0, 3, 0, 1, 0, 1), (0, 1, 2, 1, 1), (0, 1, 1, 1, 0), (1, 1, 1, 1, 0, 0, 2), (0, 0, 0, 0, 0), (2, 1), (0, 0, 2, 0, 1), (0, 1, 1, 0, 0), (1, 1, 1, 0, 0, 0, 2), (0, 1, 0, 1, 0), (0, 0, 3, 1, 2), (1, 0, 3, 1, 2, 0, 1), (1, 0, 3, 1, 2, 0, 2), (0, 0, 2, 1, 1), (0, 0, 1, 0, 1), (1, 0, 1, 0, 1, 0, 1), (1, 0, 1, 0, 1, 0, 2), (0, 0, 1, 1, 0), (1, 0, 1, 1, 0, 0, 2)),
         ((0, 1, 2, 0, 1),),
-        ((0, 0, 0, 1, 0), (0, 0, 1, 1, 1), (1, 0, 1, 1, 1, 1, 3), (1, 0, 1, 1, 1, 0, 2), (0, 1, 0, 0, 0)),
+        ((0, 0, 0, 1, 0), (2, 2), (3,), (0, 0, 1, 1, 1), (1, 0, 1, 1, 1, 1, 3), (1, 0, 1, 1, 1, 0, 2), (0, 1, 0, 0, 0)),
         ((0, 1, 1, 0, 1), (1, 1, 1, 0, 1, 0, 2), (0, 1, 0, 1, 1), (0, 1, 1, 1, 1), (1, 1, 1, 1, 1, 0, 2)),
         ((0, 1, 3, 0, 1), (1, 1, 3, 0, 1, 1, 2), (1, 1, 3, 0, 1, 0, 2), (0, 0, 1, 1, 2), (1, 0, 1, 1, 2, 0, 0), (0, 0, 0, 1, 1), (0, 0, 0, 0, 1), (0, 1, 3, 1, 1), (1, 1, 3, 1, 1, 0, 2)),
         ((0, 1, 0, 0, 1),),
     ),
 )
+STAGE_TWO = 5
 ORDER = ((7, 6, 4, 5, 10, 11, 9), (0, 7, 5, 6, 11, 4, 10), (6, 0, 1, 4, 5, 7, 11), (2, 1, 6, 0, 5, 7, 4))
-SPREAD = (1, 2, 3)
 
 
 def slot_of(age, home):
@@ -81,10 +82,11 @@
     scaling = HD ** (-0.5) * math.log2(math.e)
 
     def kernel(
-        q_ref, ck_ref, cv_ref, nk_ref, nv_ref, fill_ref, pos_ref, dest_ref,
-        out_ref, ak_ref, av_ref,
-        qt_ref, kb, vb, nvt, acc, m_ref, obuf, arecv, pk, w1, w2, app,
-        ss, rs, a_s, a_r, w1s, w1r, w2s, w2r, spread,
+        q_hbm, ck_hbm, cv_hbm, nk_hbm, nv_hbm, fill_hbm, pos_hbm, dest_hbm,
+        arecv, app,
+        q_ref, ck_ref, cv_ref, fill_ref, pos_ref, dest_ref, inverse,
+        qt_ref, kb, vb, nvt, acc, m_ref, obuf, pk, w1, w2,
+        load, ss, rs, a_s, a_r, w1s, w1r, w2s, w2r, spread,
     ):
         me = lax.axis_index("ctx")
         head = lax.axis_index("kvh")
@@ -100,6 +102,20 @@
         near += [(me, lax.rem(head + i, n_kvh)) for i in range(1, n_kvh)]
         for device in near:
             pl.semaphore_signal(barrier, inc=1, device_id=device, device_id_type=MESH)
+
+        half = pieces // 2
+        loads = [
+            pltpu.make_async_copy(src, dst, load.at[i])
+            for i, (src, dst) in enumerate((
+                (fill_hbm, fill_ref), (ck_hbm, ck_ref), (cv_hbm, cv_ref), (dest_hbm, dest_ref),
+                (nk_hbm, pk.at[pl.ds(0, half)]), (nv_hbm, pk.at[pl.ds(half, half)]),
+                (q_hbm, q_ref), (pos_hbm, pos_ref),
+            ))
+        ]
+        for copy in loads:
+            copy.start()
+        for copy in loads[:4]:
+            copy.wait()
 
         own = role
         live = fill_ref[me]
@@ -110,9 +126,16 @@
         for c in range(2):
             kb[own, c] = keys[c * HALF:(c + 1) * HALF]
             vb[own, c, 0:HD, :] = values[c * HALF:(c + 1) * HALF].T.astype(BF)
-        for i in range(pieces // 2):
-            pk[i] = nk_ref[i]
-            pk[i + pieces // 2] = nv_ref[i]
+
+        @pl.loop(0, n_ctx)
+        def _(d):
+            source = jnp.int32(0)
+            for g in range(n_ctx):
+                source = jnp.maximum(source, jnp.where(dest_ref[g] == d, g, 0))
+            inverse[d] = source
+
+        for copy in loads[4:]:
+            copy.wait()
 
         pl.semaphore_wait(barrier, len(near))
 
@@ -144,6 +167,10 @@
                     device_id=at(0, role ^ 1),
                     device_id_type=MESH,
                 ).wait_recv()
+            elif action[0] == 2:
+                spread_round(action[1])
+            elif action[0] == 3:
+                stage_one()
             else:
                 done = sends.setdefault(r, [])
                 remote(*action[1:], len(done)).start()
@@ -167,7 +194,7 @@
             qt_ref[:, b * 128:(b + 1) * 128] = block.astype(F32).T.astype(BF)
         row16 = lax.broadcasted_iota(jnp.int32, (16, HALF), 0)
         lane16 = lax.broadcasted_iota(jnp.int32, (16, HALF), 1)
-        nvt[0:HD, :] = nv_ref[...].reshape(SPAN, HD).astype(F32).T.astype(BF)
+        nvt[0:HD, :] = pk[half:pieces].reshape(SPAN, HD).astype(F32).T.astype(BF)
         nvt[HD:VROWS, :] = jnp.where(row16[:, :SPAN] == 0, 1.0, 0.0).astype(BF)
         for age in range(3):
             for j in range(4):
@@ -190,19 +217,20 @@
 
         tiles = (GROUP * SPAN) // LANES
 
-        for tile in range(tiles):
+        def own_scores(tile):
+            s = dot(pk[0:half].reshape(SPAN, HD), qt_ref[:, lanes_of(tile)])
+            row = lax.broadcasted_iota(jnp.int32, (SPAN, LANES), 0)
+            return jnp.where(row <= tokens(tile, SPAN), s, -1e30)
+
+        def own_absorb(tile, s):
             lanes = lanes_of(tile)
-            s = dot(nk_ref[...].reshape(SPAN, HD), qt_ref[:, lanes])
-            row = lax.broadcasted_iota(jnp.int32, (SPAN, LANES), 0)
-            s = jnp.where(row <= tokens(tile, SPAN), s, -1e30)
             top = jnp.max(s, axis=0, keepdims=True)
             weights = jnp.exp2((s - top) * scaling).astype(BF)
             acc[:, lanes] = dot(nvt[...], weights)
             m_ref[:, lanes] = top
 
-        def attend(tile, slot, home):
-            lanes = lanes_of(tile)
-            qt = qt_ref[:, lanes]
+        def shard_scores(slot, home, tile):
+            qt = qt_ref[:, lanes_of(tile)]
             parts = []
             for c in range(2):
                 s = dot(kb[slot, c], qt)
@@ -210,6 +238,10 @@
                     row = lax.broadcasted_iota(jnp.int32, (HALF, LANES), 0) + c * HALF
                     s = jnp.where(row <= tokens(tile, HALF) + pos_ref[0], s, -1e30)
                 parts.append(s)
+            return parts
+
+        def shard_absorb(slot, tile, parts):
+            lanes = lanes_of(tile)
             old = m_ref[:, lanes]
             top = jnp.maximum(old, jnp.max(jnp.maximum(parts[0], parts[1]), axis=0, keepdims=True))
             total = acc[:, lanes] * jnp.exp2((old - top) * scaling)
@@ -219,8 +251,22 @@
             acc[:, lanes] = total
             m_ref[:, lanes] = top
 
-        for tile in range(tiles):
-            attend(tile, own, True)
+        def in_turn(order, scores, absorb, after=None):
+            ahead = [scores(tile) for tile in order[:AHEAD]]
+            for i, tile in enumerate(order):
+                if i + AHEAD < len(order):
+                    ahead.append(scores(order[i + AHEAD]))
+                absorb(tile, ahead.pop(0))
+                if after is not None:
+                    after(i, tile)
+
+        def attend(slot, home=False, order=tuple(range(tiles)), after=None):
+            in_turn(
+                order, functools.partial(shard_scores, slot, home), functools.partial(shard_absorb, slot), after
+            )
+
+        in_turn(tuple(range(tiles)), own_scores, own_absorb)
+        attend(own, home=True)
 
         def spread_round(k):
             pl.semaphore_wait(spread.at[k], 2)
@@ -253,10 +299,7 @@
 
             @pl.loop(0, n_ctx)
             def _(d):
-                source = jnp.int32(0)
-                for g in range(n_ctx):
-                    source = jnp.maximum(source, jnp.where(dest_ref[g] == d, g, 0))
-                w2[d] = w1[source]
+                w2[d] = w1[inverse[d]]
 
             app[me] = w2[me]
 
@@ -274,16 +317,7 @@
                             def _(i=i):
                                 for action in SEQ[r][i]:
                                     act(r, action)
-            for k in range(3):
-                @pl.when(step == SPREAD[k])
-                def _(k=k):
-                    spread_round(k)
-
-            @pl.when(step == SPREAD[2])
-            def _():
-                stage_one()
-
-            @pl.when(step == 6)
+            @pl.when(step == STAGE_TWO)
             def _():
                 stage_two()
 
@@ -300,8 +334,7 @@
         def _(step):
             communicate(step)
             slot = slot_at(step)
-            for tile in range(tiles):
-                attend(tile, slot, False)
+            attend(slot)
 
         communicate(6)
         last = slot_at(6)
@@ -324,21 +357,21 @@
                 def _():
                     arecv[b] = obuf[b]
 
-        previous = None
-        for i in range(tiles):
-            tile = lax.rem(head // 2 + 1 + i, tiles)
-            attend(tile, last, False)
+        turn = [lax.rem(head // 2 + 1 + i, tiles) for i in range(tiles)]
+
+        def finish(i, tile):
             lanes = lanes_of(tile)
             result = acc[0:HD, lanes] * (1.0 / acc[HD:HD + 1, lanes])
             result = result.T.astype(BF)
-            for half in range(2):
+            for part in range(2):
                 for g in range(GROUP):
-                    at_row = half * 128 + g * 16
-                    obuf[tile * 2 + half, :, g * HD:(g + 1) * HD] = result[at_row:at_row + 16]
-            if previous is not None:
-                ship(previous)
-            previous = tile
-        ship(previous)
+                    at_row = part * 128 + g * 16
+                    obuf[tile * 2 + part, :, g * HD:(g + 1) * HD] = result[at_row:at_row + 16]
+            if i > 0:
+                ship(turn[i - 1])
+
+        attend(last, order=turn, after=finish)
+        ship(turn[-1])
 
         for k in range(1, n_kvh):
             h = lax.rem(head + k, n_kvh)
@@ -346,17 +379,10 @@
                 src_ref=obuf.at[h], dst_ref=arecv.at[h], send_sem=a_s.at[h], recv_sem=a_r.at[h],
                 device_id=(me, h), device_id_type=MESH,
             ).wait()
-        for h in range(n_kvh):
-            out_ref[:, h * GROUP * HD:(h + 1) * GROUP * HD] = arecv[h]
-
         @pl.loop(1, n_ctx)
         def _(k):
             d = other(k)
             stage_copy(w2.at[d], app.at[d], w2s, w2r, d, k, d).wait()
-
-        for i in range(pieces // 2):
-            ak_ref[i] = app[i]
-            av_ref[i] = app[i + pieces // 2]
 
         for r in range(4):
             @pl.when(role == r)
@@ -367,18 +393,23 @@
     half = pieces // 2
     rows8 = SPAN // half
     vmem = pl.BlockSpec(memory_space=pltpu.VMEM)
-    smem = pl.BlockSpec(memory_space=pltpu.SMEM)
     dma = pltpu.SemaphoreType.DMA
-    attn, keys, values = pl.pallas_call(
+    blocks, spans = pl.pallas_call(
         kernel,
         out_shape=(
-            jax.ShapeDtypeStruct((SPAN // n_kvh, n_kvh * GROUP * HD), BF),
-            jax.ShapeDtypeStruct((half, rows8, HD), BF),
-            jax.ShapeDtypeStruct((half, rows8, HD), BF),
+            jax.ShapeDtypeStruct((n_kvh, SPAN // n_kvh, GROUP * HD), BF),
+            jax.ShapeDtypeStruct((pieces, rows8, HD), BF),
         ),
-        in_specs=[vmem] * 5 + [smem] * 3,
-        out_specs=(vmem, vmem, vmem),
+        in_specs=[pl.BlockSpec(memory_space=pl.ANY)] * 8,
+        out_specs=(vmem, vmem),
         scratch_shapes=[
+            pltpu.VMEM((SPAN, GROUP * HD), BF),
+            pltpu.VMEM((SHARD, HD), BF),
+            pltpu.VMEM((SHARD, HD), BF),
+            pltpu.SMEM((n_ctx,), jnp.int32),
+            pltpu.SMEM((1,), jnp.int32),
+            pltpu.SMEM((n_ctx,), jnp.int32),
+            pltpu.SMEM((n_ctx,), jnp.int32),
             pltpu.VMEM((HD, GROUP * SPAN), BF),
             pltpu.VMEM((12, 2, HALF, HD), BF),
             pltpu.VMEM((12, 2, VROWS, HALF), BF),
@@ -386,11 +417,10 @@
             pltpu.VMEM((VROWS, GROUP * SPAN), F32),
             pltpu.VMEM((1, GROUP * SPAN), F32),
             pltpu.VMEM((n_kvh, SPAN // n_kvh, GROUP * HD), BF),
-            pltpu.VMEM((n_kvh, SPAN // n_kvh, GROUP * HD), BF),
             pltpu.VMEM((pieces, rows8, HD), BF),
             pltpu.VMEM((pieces, rows8, HD), BF),
             pltpu.VMEM((pieces, rows8, HD), BF),
-            pltpu.VMEM((pieces, rows8, HD), BF),
+            dma((8,)),
             dma((48,)),
             dma((2, 12, 2)),
             dma((n_kvh,)),
@@ -408,6 +438,25 @@
         new_keys.reshape(half, rows8, HD), new_values.reshape(half, rows8, HD),
         cache_fill, span_pos, destination,
     )
+
+    def place(blocks_ref, spans_ref, out_ref, ak_ref, av_ref):
+        for h in range(n_kvh):
+            out_ref[:, h * GROUP * HD:(h + 1) * GROUP * HD] = blocks_ref[h]
+        for i in range(half):
+            ak_ref[i] = spans_ref[i]
+            av_ref[i] = spans_ref[i + half]
+
+    attn, keys, values = pl.pallas_call(
+        place,
+        out_shape=(
+            jax.ShapeDtypeStruct((SPAN // n_kvh, n_kvh * GROUP * HD), BF),
+            jax.ShapeDtypeStruct((half, rows8, HD), BF),
+            jax.ShapeDtypeStruct((half, rows8, HD), BF),
+        ),
+        in_specs=[vmem] * 2,
+        out_specs=(vmem,) * 3,
+        name="place_outputs",
+    )(blocks, spans)
     return attn, keys.reshape(SPAN, HD), values.reshape(SPAN, HD)
 
 

time: 49 us -> 42.2 us (0.86)
  the two profiles are of different devices: /device:TPU:1 before, /device:TPU:8 now
where the time goes in v2:
time: 42.2 us; the launch traced here: 42.1 us
  Pallas kernels  40.8 us (97%)
  between operations  1.29 us (3%)
    pallas_call x1, Pallas kernels, per_device(): pl.pallas_call(kernel, out_shape=(jax.ShapeDtypeStruct((n_kvh, SPAN // n_...  39.1 us
    pallas_call x1, Pallas kernels, per_device(): pl.pallas_call(place, out_shape=(jax.ShapeDtypeStruct((SPAN // n_kvh, n_k...  1.68 us

profile of v2, /device:TPU:8, one launch (start us, length us, event | category | flops | bytes accessed | tf_op | source)
XLA Modules:
  0.0 42.1 jit_solution(10813719225644894654)
XLA Ops:
  1.3 39.1 %spanned_attention.1 = (bf16[8,16,1024]{2,1,0:T(8,128)(2,1)}, bf16[32,8,128]{2,1,0:T(8,128)(2,1)}) custom-call(bf16[128,1024]{1,0:T(8,128)(2,1)} %q_hbm.1, bf16[512,128]{1,0:T(8,128)(2,1)} %ck_hbm.1, bf16[512,128]{1,0:T(8,128)(2,1)} %cv_hbm.1, bf16[16,8,128]{2,1,0:T(8,128)(2,1)} %bitcast.4, bf16[16,8,128]{2,1,0:T(8,128)(2,1)} %bitcast.5, s32[32]{0:T(128)} %fill_hbm.1, ...), custom_call_target="tpu_custom_call" | custom-call | tf_op jit(solution)/shard_map/spanned_attention/pallas_call | solution.py:397
  40.4 1.7 %place_outputs.1 = (bf16[16,8192]{1,0:T(8,128)(2,1)}, bf16[16,8,128]{2,1,0:T(8,128)(2,1)}, bf16[16,8,128]{2,1,0:T(8,128)(2,1)}) custom-call(bf16[8,16,1024]{2,1,0:T(8,128)(2,1)} %get-tuple-element.8.blocks_ref, bf16[32,8,128]{2,1,0:T(8,128)(2,1)} %get-tuple-element.9.spans_ref), custom_call_target="tpu_custom_call" | custom-call | tf_op jit(solution)/shard_map/place_outputs/pallas_call | solution.py:449

commit v3 on v2

v3 whole, which is shorter than its diff:
```python
import functools
import math

import jax
import jax.numpy as jnp
from jax import lax
from jax.experimental import pallas as pl
from jax.experimental.pallas import tpu as pltpu
from jax.sharding import PartitionSpec as P

MESH = pl.DeviceIdType.MESH
SPAN = 128
HD = 128
GROUP = 8
SHARD = 512
HALF = 256
LANES = 256
VROWS = 144
AHEAD = 4
PAIR_AHEAD = 1
SINGLE = 3
BF = jnp.bfloat16
F32 = jnp.float32

FIRST = (
    ((1, 1, 0, 0, 0, 0, 3), (1, 0, 0, 0, 0, 1, 0), (1, 0, 0, 1, 0, 0, 3), (1, 1, 0, 0, 0, 0, 1), (1, 1, 0, 1, 0, 0, 2), (1, 1, 0, 0, 0, 1, 1), (1, 1, 0, 1, 0, 0, 1), (1, 0, 0, 1, 0, 1, 1), (1, 0, 0, 0, 0, 0, 2), (1, 0, 0, 0, 0, 0, 1), (1, 0, 0, 1, 0, 0, 1), (1, 1, 0, 1, 0, 1, 0)),
    ((1, 1, 1, 1, 0, 0, 3), (1, 1, 1, 0, 0, 1, 1), (1, 0, 1, 1, 0, 0, 3), (1, 0, 1, 0, 0, 0, 3), (1, 1, 1, 0, 0, 0, 3)),
    ((1, 1, 2, 0, 0, 1, 3), (1, 1, 2, 1, 0, 0, 3), (1, 0, 2, 1, 0, 0, 3), (1, 1, 2, 0, 0, 0, 3), (1, 1, 2, 1, 0, 1, 3), (1, 0, 2, 0, 0, 0, 3), (1, 0, 2, 1, 0, 1, 3), (1, 0, 2, 0, 0, 1, 3)),
    ((1, 0, 3, 1, 0, 0, 1), (1, 0, 3, 0, 0, 0, 1), (1, 1, 3, 0, 0, 1, 3), (1, 1, 3, 1, 0, 0, 1)),
)
SEQ = (
    (
        ((2, 0), (0, 0, 0, 0, 1), (1, 0, 0, 0, 1, 0, 2), (1, 0, 0, 0, 1, 0, 1), (5, 0), (2, 1), (0, 1, 0, 1, 1), (1, 1, 0, 1, 1, 0, 1), (0, 1, 0, 0, 1), (0, 0, 0, 1, 1)),
        ((0, 0, 3, 1, 1), (0, 1, 3, 0, 1), (0, 0, 3, 0, 1), (0, 1, 3, 1, 1)),
        ((0, 1, 2, 0, 1), (0, 1, 2, 1, 1), (2, 2), (3,), (5, 1), (0, 0, 2, 1, 1), (0, 0, 2, 0, 1)),
        ((0, 0, 3, 1, 2), (0, 0, 3, 0, 2), (0, 1, 3, 0, 2), (0, 1, 3, 1, 2)),
        ((0, 1, 1, 0, 1), (0, 1, 1, 1, 1), (0, 0, 1, 1, 1), (0, 0, 1, 0, 1)),
        ((0, 1, 2, 0, 2), (0, 1, 2, 1, 2), (0, 0, 2, 1, 2), (0, 0, 2, 0, 2)),
        ((0, 0, 1, 1, 2), (0, 1, 1, 1, 2), (0, 0, 1, 0, 2), (0, 1, 1, 0, 2)),
    ),
    (
        ((0, 1, 0, 0, 0), (0, 1, 0, 1, 0), (0, 0, 0, 0, 0), (0, 0, 0, 1, 0)),
        ((0, 1, 1, 0, 1), (1, 1, 1, 0, 1, 0, 3), (1, 1, 1, 0, 1, 0, 0), (0, 0, 3, 1, 0), (1, 0, 3, 1, 0, 1, 1), (2, 0), (0, 0, 3, 0, 0), (1, 0, 3, 0, 0, 1, 1), (0, 1, 0, 0, 1), (1, 1, 0, 0, 1, 0, 0), (1, 1, 0, 0, 1, 0, 3), (0, 1, 3, 1, 0), (1, 1, 3, 1, 0, 1, 1), (5, 0), (0, 0, 0, 1, 1), (1, 0, 0, 1, 1, 0, 0), (0, 0, 3, 1, 1), (1, 0, 3, 1, 1, 1, 1), (1, 0, 3, 1, 1, 0, 3), (1, 0, 3, 1, 1, 0, 0), (0, 1, 3, 0, 1), (1, 1, 3, 0, 1, 0, 0), (2, 1), (0, 0, 3, 0, 1), (1, 0, 3, 0, 1, 0, 3), (1, 0, 3, 0, 1, 1, 1), (1, 0, 3, 0, 1, 0, 0), (0, 1, 2, 0, 1), (1, 1, 2, 0, 1, 0, 0), (1, 1, 2, 0, 1, 1, 1), (0, 1, 3, 1, 1), (1, 1, 3, 1, 1, 1, 1), (1, 1, 3, 1, 1, 0, 3), (1, 1, 3, 1, 1, 0, 0), (0, 1, 2, 1, 1), (1, 1, 2, 1, 1, 0, 0), (1, 1, 2, 1, 1, 1, 1)),
        ((0, 0, 3, 1, 2), (1, 0, 3, 1, 2, 0, 2), (1, 0, 3, 1, 2, 0, 0), (0, 0, 2, 1, 1), (1, 0, 2, 1, 1, 1, 1), (1, 0, 2, 1, 1, 0, 0), (0, 0, 0, 0, 1), (0, 1, 0, 1, 1)),
        ((0, 0, 3, 0, 2), (1, 0, 3, 0, 2, 0, 0), (0, 1, 3, 0, 2), (1, 1, 3, 0, 2, 0, 0), (2, 2), (3,), (5, 1), (0, 1, 2, 0, 2), (1, 1, 2, 0, 2, 0, 0), (0, 0, 2, 0, 1), (1, 0, 2, 0, 1, 0, 0), (1, 0, 2, 0, 1, 1, 1)),
        ((0, 1, 3, 1, 2), (1, 1, 3, 1, 2, 0, 2), (1, 1, 3, 1, 2, 0, 0), (0, 1, 1, 1, 1), (1, 1, 1, 1, 1, 0, 0), (1, 1, 1, 1, 1, 1, 0)),
        ((0, 1, 2, 1, 2), (1, 1, 2, 1, 2, 0, 0), (0, 0, 1, 1, 1), (1, 0, 1, 1, 1, 0, 0), (0, 0, 2, 1, 2), (1, 0, 2, 1, 2, 0, 0), (0, 0, 1, 0, 1), (1, 0, 1, 0, 1, 0, 0), (1, 0, 1, 0, 1, 1, 0)),
        ((0, 0, 2, 0, 2), (1, 0, 2, 0, 2, 0, 0)),
    ),
    (
        ((2, 0), (5, 0), (2, 1), (0, 1, 0, 1, 0), (1, 1, 0, 1, 0, 0, 3), (1, 1, 0, 1, 0, 1, 2), (0, 1, 2, 0, 1), (0, 1, 2, 1, 1), (0, 0, 2, 1, 1), (0, 0, 2, 0, 1)),
        ((2, 2), (3,), (0, 0, 0, 0, 0), (1, 0, 0, 0, 0, 0, 3), (0, 1, 0, 0, 0), (0, 0, 0, 1, 0)),
        ((0, 1, 1, 1, 0), (0, 0, 1, 1, 0), (0, 0, 1, 0, 0), (5, 1), (0, 1, 1, 0, 0)),
        ((0, 0, 0, 0, 1), (1, 0, 0, 0, 1, 0, 3), (0, 1, 1, 1, 1), (0, 0, 1, 1, 1), (0, 0, 1, 0, 1), (0, 1, 1, 0, 1)),
        ((0, 1, 0, 1, 1), (1, 1, 0, 1, 1, 0, 3), (0, 0, 0, 1, 1), (0, 1, 0, 0, 1)),
        ((0, 1, 3, 0, 1), (0, 0, 3, 1, 1), (0, 0, 3, 0, 1), (0, 1, 3, 1, 1)),
        ((0, 1, 3, 0, 2), (0, 0, 3, 1, 2), (0, 0, 3, 0, 2), (0, 1, 3, 1, 2)),
    ),
    (
        ((0, 1, 2, 1, 0), (0, 0, 2, 1, 0), (0, 1, 2, 0, 0), (0, 0, 2, 0, 0)),
        ((0, 1, 3, 0, 1), (1, 1, 3, 0, 1, 1, 3), (1, 1, 3, 0, 1, 0, 1), (1, 1, 3, 0, 1, 0, 2), (2, 0), (0, 1, 2, 0, 1), (1, 1, 2, 0, 1, 0, 2), (1, 1, 2, 0, 1, 0, 1), (0, 1, 1, 1, 0), (1, 1, 1, 1, 0, 1, 3), (1, 1, 1, 1, 0, 0, 2), (0, 1, 2, 1, 1), (1, 1, 2, 1, 1, 0, 1), (1, 1, 2, 1, 1, 0, 2), (0, 1, 0, 0, 0), (1, 1, 0, 0, 0, 0, 2), (5, 0), (0, 0, 2, 1, 1), (1, 0, 2, 1, 1, 0, 1), (1, 0, 2, 1, 1, 0, 2), (0, 0, 1, 1, 0), (1, 0, 1, 1, 0, 1, 3), (1, 0, 1, 1, 0, 0, 2), (0, 0, 0, 1, 0), (1, 0, 0, 1, 0, 0, 2), (1, 0, 0, 1, 0, 1, 3), (0, 1, 3, 0, 2), (1, 1, 3, 0, 2, 0, 1), (1, 1, 3, 0, 2, 0, 2), (2, 1), (0, 0, 2, 0, 1), (1, 0, 2, 0, 1, 0, 1), (1, 0, 2, 0, 1, 0, 2), (0, 1, 1, 1, 1), (1, 1, 1, 1, 1, 0, 2), (1, 1, 1, 1, 1, 0, 1), (0, 0, 1, 0, 0), (1, 0, 1, 0, 0, 0, 2), (1, 0, 1, 0, 0, 1, 3)),
        ((0, 0, 1, 1, 1), (1, 0, 1, 1, 1, 0, 1), (1, 0, 1, 1, 1, 1, 3), (1, 0, 1, 1, 1, 0, 2), (0, 0, 0, 1, 1), (1, 0, 0, 1, 1, 0, 2), (0, 1, 1, 0, 0), (1, 1, 1, 0, 0, 0, 2)),
        ((0, 0, 1, 0, 1), (1, 0, 1, 0, 1, 0, 1), (1, 0, 1, 0, 1, 0, 2), (2, 2), (3,), (5, 1), (0, 1, 1, 0, 1), (1, 1, 1, 0, 1, 1, 3), (1, 1, 1, 0, 1, 0, 2)),
        ((0, 0, 1, 1, 2), (1, 0, 1, 1, 2, 0, 0), (0, 1, 0, 0, 1), (1, 1, 0, 0, 1, 0, 2), (0, 1, 0, 1, 0), (0, 0, 0, 0, 0)),
        ((0, 0, 3, 1, 1), (1, 0, 3, 1, 1, 0, 2), (0, 1, 1, 0, 2), (1, 1, 1, 0, 2, 0, 0), (0, 0, 3, 0, 1), (1, 0, 3, 0, 1, 0, 2), (1, 0, 3, 0, 1, 1, 2), (0, 1, 3, 1, 1), (1, 1, 3, 1, 1, 0, 2)),
        ((0, 0, 0, 0, 1), (0, 1, 0, 1, 1)),
    ),
)
STAGE_TWO = 5
ORDER = ((4, 7, 6, 11, 5, 10, 9), (0, 7, 4, 6, 11, 5, 10), (6, 0, 1, 5, 4, 7, 11), (2, 6, 1, 5, 0, 7, 4))


def slot_of(age, home):
    return age * 4 + home


def per_device(
    queries, cache_keys, cache_values, new_keys, new_values, cache_fill, span_pos, destination
):
    n_ctx = lax.axis_size("ctx")
    n_kvh = lax.axis_size("kvh")
    planes = n_ctx // 4
    pieces = n_ctx
    scaling = HD ** (-0.5) * math.log2(math.e)

    def kernel(
        q_hbm, ck_hbm, cv_hbm, nk_hbm, nv_hbm, fill_hbm, pos_hbm, dest_hbm,
        arecv, app,
        q_ref, ck_ref, cv_ref, fill_ref, pos_ref, dest_ref, inverse,
        qt_ref, kb, vb, nvt, acc, m_ref, obuf, pk, w1, w2,
        load, ss, rs, a_s, a_r, w_s, w_r, home, spread, across,
    ):
        me = lax.axis_index("ctx")
        head = lax.axis_index("kvh")
        plane = me // 4
        role = lax.rem(me, 4)

        def at(up, r):
            return (lax.rem(plane + up + planes, planes) * 4 + r, head)

        barrier = pltpu.get_barrier_semaphore()
        near = [at(0, role ^ 1), at(0, role ^ 2), at(0, role ^ 3)]
        near += [at(1, role), at(-1, role), at(1, role ^ 1), at(-1, role ^ 1)]
        beside = [(me, lax.rem(head + 2, n_kvh)), (me, lax.rem(head + n_kvh - 2, n_kvh)), (me, head ^ 1)]
        near += beside
        for device in near:
            pl.semaphore_signal(barrier, inc=1, device_id=device, device_id_type=MESH)

        half = pieces // 2
        loads = [
            pltpu.make_async_copy(src, dst, load.at[i])
            for i, (src, dst) in enumerate((
                (fill_hbm, fill_ref), (ck_hbm, ck_ref), (cv_hbm, cv_ref), (dest_hbm, dest_ref),
                (nk_hbm, pk.at[pl.ds(0, half)]), (nv_hbm, pk.at[pl.ds(half, half)]),
                (q_hbm, q_ref), (pos_hbm, pos_ref),
            ))
        ]
        for copy in loads:
            copy.start()
        for copy in loads[:3]:
            copy.wait()

        own = role
        live = fill_ref[me]
        keys = ck_ref[...].astype(F32)
        alive = lax.broadcasted_iota(jnp.int32, (SHARD, HD), 0) < live
        keys = jnp.where(alive, keys, keys[0:1, :]).astype(BF)
        values = jnp.where(alive, cv_ref[...].astype(F32), 0.0)
        for c in range(2):
            kb[own * 2 + c] = keys[c * HALF:(c + 1) * HALF]
            vb[own * 2 + c, 0:HD, :] = values[c * HALF:(c + 1) * HALF].T.astype(BF)

        for copy in loads[3:]:
            copy.wait()

        pl.semaphore_wait(barrier, len(near))

        def piece(t, j, c, age):
            if t == 0:
                return kb.at[slot_of(age, j) * 2 + c]
            return vb.at[slot_of(age, j) * 2 + c, pl.ds(0, HD)]

        def remote(t, j, c, age, up, r):
            return pltpu.make_async_remote_copy(
                src_ref=piece(t, j, c, age),
                dst_ref=piece(t, j, c, age + up),
                send_sem=ss.at[t],
                recv_sem=rs.at[t, slot_of(age + up, j), c],
                device_id=at(up, r),
                device_id_type=MESH,
            )

        def act(action):
            if action[0] == 0:
                _, t, j, c, age = action
                pltpu.make_async_remote_copy(
                    src_ref=piece(t, j, c, age),
                    dst_ref=piece(t, j, c, age),
                    send_sem=ss.at[t],
                    recv_sem=rs.at[t, slot_of(age, j), c],
                    device_id=at(0, role ^ 1),
                    device_id_type=MESH,
                ).wait_recv()
            elif action[0] == 2:
                spread_round(action[1])
            elif action[0] == 5:
                pl.semaphore_wait(across.at[action[1]], 3)
                if action[1] == 0:
                    signal_beside(1)
            elif action[0] == 3:
                stage_one()
            else:
                remote(*action[1:]).start()

        for r in range(4):
            @pl.when(role == r)
            def _(r=r):
                for action in FIRST[r]:
                    act(action)

        def signal_planes(k, step):
            for up in (step, -step):
                pl.semaphore_signal(spread.at[k], inc=1, device_id=at(up, role), device_id_type=MESH)

        def signal_beside(k):
            for device in beside:
                pl.semaphore_signal(across.at[k], inc=1, device_id=device, device_id_type=MESH)

        signal_planes(0, 1)
        signal_beside(0)

        @pl.loop(0, n_ctx)
        def _(d):
            source = jnp.int32(0)
            for g in range(n_ctx):
                source = jnp.maximum(source, jnp.where(dest_ref[g] == d, g, 0))
            inverse[d] = source

        for b in range(SPAN // 16):
            rows = [q_ref[b * 16:(b + 1) * 16, g * HD:(g + 1) * HD] for g in range(GROUP)]
            block = jnp.concatenate(rows, axis=0)
            qt_ref[:, b * 128:(b + 1) * 128] = block.astype(F32).T.astype(BF)
        row16 = lax.broadcasted_iota(jnp.int32, (16, HALF), 0)
        lane16 = lax.broadcasted_iota(jnp.int32, (16, HALF), 1)
        nvt[0:HD, :] = pk[half:pieces].reshape(SPAN, HD).astype(F32).T.astype(BF)
        nvt[HD:VROWS, :] = jnp.where(row16[:, :SPAN] == 0, 1.0, 0.0).astype(BF)
        for age in range(3):
            for j in range(4):
                filled = fill_ref[at(-age, j)[0]]
                for c in range(2):
                    seen = (row16 == 0) & (lane16 + c * HALF < filled)
                    vb[slot_of(age, j) * 2 + c, HD:VROWS, :] = jnp.where(seen, 1.0, 0.0).astype(BF)

        def tokens(tile, rows):
            lane = lax.broadcasted_iota(jnp.int32, (rows, LANES), 1)
            return (tile * 2 + lane // 128) * 16 + lane % 16

        def dot(a, b):
            return jnp.dot(a, b, preferred_element_type=F32)

        def lanes_of(tile):
            if isinstance(tile, int):
                return pl.ds(tile * LANES, LANES)
            return pl.ds(pl.multiple_of(tile * LANES, LANES), LANES)

        tiles = (GROUP * SPAN) // LANES

        def own_scores(tile):
            s = dot(pk[0:half].reshape(SPAN, HD), qt_ref[:, lanes_of(tile)])
            row = lax.broadcasted_iota(jnp.int32, (SPAN, LANES), 0)
            return jnp.where(row <= tokens(tile, SPAN), s, -1e30)

        def own_absorb(tile, s):
            lanes = lanes_of(tile)
            top = jnp.max(s, axis=0, keepdims=True)
            weights = jnp.exp2((s - top) * scaling).astype(BF)
            acc[:, lanes] = dot(nvt[...], weights)
            m_ref[:, lanes] = top

        def shard_scores(slots, home, tile):
            qt = qt_ref[:, lanes_of(tile)]
            parts = []
            for slot in slots:
                for c in range(2):
                    s = dot(kb[slot * 2 + c], qt)
                    if home:
                        row = lax.broadcasted_iota(jnp.int32, (HALF, LANES), 0) + c * HALF
                        s = jnp.where(row <= tokens(tile, HALF) + pos_ref[0], s, -1e30)
                    parts.append(s)
            return parts

        def shard_absorb(slots, tile, parts):
            lanes = lanes_of(tile)
            old = m_ref[:, lanes]
            top = jnp.maximum(old, jnp.max(functools.reduce(jnp.maximum, parts), axis=0, keepdims=True))
            total = acc[:, lanes] * jnp.exp2((old - top) * scaling)
            for i, part in enumerate(parts):
                weights = jnp.exp2((part - top) * scaling).astype(BF)
                total = total + dot(vb[slots[i // 2] * 2 + i % 2], weights)
            acc[:, lanes] = total
            m_ref[:, lanes] = top

        def in_turn(order, scores, absorb, after=None, depth=AHEAD):
            ahead = [scores(tile) for tile in order[:depth]]
            for i, tile in enumerate(order):
                if i + depth < len(order):
                    ahead.append(scores(order[i + depth]))
                absorb(tile, ahead.pop(0))
                if after is not None:
                    after(i, tile)

        def attend(slots, home=False, order=tuple(range(tiles)), after=None):
            in_turn(
                order,
                functools.partial(shard_scores, slots, home),
                functools.partial(shard_absorb, slots),
                after,
                AHEAD if len(slots) == 1 else PAIR_AHEAD,
            )

        in_turn(tuple(range(tiles)), own_scores, own_absorb)
        attend((own,), home=True)

        def spread_round(k):
            pl.semaphore_wait(spread.at[k], 2)
            if k == 0:
                signal_planes(1, 2)
            elif k == 1:
                signal_planes(2, 1)

        def stage_copy(src, dst, stage, device):
            return pltpu.make_async_remote_copy(
                src_ref=src, dst_ref=dst, send_sem=w_s.at[stage], recv_sem=w_r.at[stage],
                device_id=(device, head), device_id_type=MESH,
            )

        def stage_wait(src, dst, stage):
            most = pl.ds(0, n_ctx - 1)
            stage_copy(src.at[most], dst.at[most], stage, me ^ 1).wait()

        def other(k):
            return lax.rem(me + k, n_ctx)

        def stage_one():
            w1[me] = pk[me]

            @pl.loop(1, n_ctx)
            def _(k):
                stage_copy(pk.at[other(k)], w1.at[me], 0, other(k)).start()

        def stage_two():
            stage_wait(pk, w1, 0)

            @pl.loop(0, n_ctx)
            def _(d):
                w2[d] = w1[inverse[d]]

            pltpu.make_async_copy(w2.at[me], app.at[me], home.at[1]).start()

            @pl.loop(1, n_ctx)
            def _(k):
                stage_copy(w2.at[other(k)], app.at[me], 1, other(k)).start()

        def communicate(step):
            for r in range(4):
                @pl.when(role == r)
                def _(r=r):
                    for i in range(7) if not isinstance(step, int) else (step,):
                        if not isinstance(step, int):
                            if i >= SINGLE:
                                continue

                            @pl.when(step == i)
                            def _(i=i):
                                for action in SEQ[r][i]:
                                    act(action)
                        else:
                            for action in SEQ[r][i]:
                                act(action)
            if isinstance(step, int) and step == STAGE_TWO:
                stage_two()

        def slot_at(step):
            slot = jnp.int32(0)
            for r in range(4):
                code = jnp.int32(ORDER[r][0])
                for i in range(1, 7):
                    code = jnp.where(step == i, ORDER[r][i], code)
                slot = jnp.where(role == r, code, slot)
            return slot

        @pl.loop(0, SINGLE)
        def _(step):
            communicate(step)
            attend((slot_at(step),))

        for step in range(SINGLE, 5, 2):
            communicate(step)
            communicate(step + 1)
            attend((slot_at(step), slot_at(step + 1)))

        communicate(5)
        communicate(6)
        last = (slot_at(5), slot_at(6))

        def out_copy(b):
            return pltpu.make_async_remote_copy(
                src_ref=obuf.at[b], dst_ref=arecv.at[head], send_sem=a_s.at[b], recv_sem=a_r.at[head],
                device_id=(me, b), device_id_type=MESH,
            )

        def ship(tile):
            for half in range(2):
                b = tile * 2 + half

                @pl.when(b != head)
                def _():
                    out_copy(b).start()

                @pl.when(b == head)
                def _():
                    pltpu.make_async_copy(obuf.at[b], arecv.at[b], home.at[0]).start()

        turn = [lax.rem(head // 2 + i, tiles) for i in (2, 1, 3, 0)]

        def finish(i, tile):
            lanes = lanes_of(tile)
            result = acc[0:HD, lanes] * (1.0 / acc[HD:HD + 1, lanes])
            result = result.T.astype(BF)
            for part in range(2):
                for g in range(GROUP):
                    at_row = part * 128 + g * 16
                    obuf[tile * 2 + part, :, g * HD:(g + 1) * HD] = result[at_row:at_row + 16]
            if i > 0:
                ship(turn[i - 1])

        attend(last, order=turn, after=finish)
        ship(turn[-1])
        if STAGE_TWO == 7:
            stage_two()

        for k in range(1, n_kvh):
            h = lax.rem(head + k, n_kvh)
            pltpu.make_async_remote_copy(
                src_ref=obuf.at[h], dst_ref=arecv.at[h], send_sem=a_s.at[h], recv_sem=a_r.at[h],
                device_id=(me, h), device_id_type=MESH,
            ).wait()
        stage_wait(w2, app, 1)
        pltpu.make_async_copy(obuf.at[head], arecv.at[head], home.at[0]).wait()
        pltpu.make_async_copy(w2.at[me], app.at[me], home.at[1]).wait()

        for r in range(4):
            @pl.when(role == r)
            def _(r=r):
                for t in range(2):
                    actions = FIRST[r] + sum(SEQ[r], ())
                    count = sum(a[:2] == (1, t) for a in actions)
                    whole = kb.at[pl.ds(0, count)] if t == 0 else vb.at[pl.ds(0, count), pl.ds(0, HD)]
                    pltpu.make_async_remote_copy(
                        src_ref=whole, dst_ref=whole, send_sem=ss.at[t], recv_sem=rs.at[0, 0, 0],
                        device_id=at(0, role ^ 1), device_id_type=MESH,
                    ).wait_send()

    half = pieces // 2
    rows8 = SPAN // half
    dma = pltpu.SemaphoreType.DMA
    blocks, spans = pl.pallas_call(
        kernel,
        out_shape=(
            jax.ShapeDtypeStruct((n_kvh, SPAN // n_kvh, GROUP * HD), BF),
            jax.ShapeDtypeStruct((pieces, rows8, HD), BF),
        ),
        in_specs=[pl.BlockSpec(memory_space=pl.ANY)] * 6
        + [pl.BlockSpec(memory_space=pltpu.HBM), pl.BlockSpec(memory_space=pl.ANY)],
        out_specs=(pl.BlockSpec(memory_space=pl.ANY),) * 2,
        scratch_shapes=[
            pltpu.VMEM((SPAN, GROUP * HD), BF),
            pltpu.VMEM((SHARD, HD), BF),
            pltpu.VMEM((SHARD, HD), BF),
            pltpu.SMEM((n_ctx,), jnp.int32),
            pltpu.SMEM((1,), jnp.int32),
            pltpu.SMEM((n_ctx,), jnp.int32),
            pltpu.SMEM((n_ctx,), jnp.int32),
            pltpu.VMEM((HD, GROUP * SPAN), BF),
            pltpu.VMEM((24, HALF, HD), BF),
            pltpu.VMEM((24, VROWS, HALF), BF),
            pltpu.VMEM((VROWS, SPAN), BF),
            pltpu.VMEM((VROWS, GROUP * SPAN), F32),
            pltpu.VMEM((1, GROUP * SPAN), F32),
            pltpu.VMEM((n_kvh, SPAN // n_kvh, GROUP * HD), BF),
            pltpu.VMEM((pieces, rows8, HD), BF),
            pltpu.VMEM((pieces, rows8, HD), BF),
            pltpu.VMEM((pieces, rows8, HD), BF),
            dma((8,)),
            dma((2,)),
            dma((2, 12, 2)),
            dma((n_kvh,)),
            dma((n_kvh,)),
            dma((2,)),
            dma((2,)),
            dma((2,)),
            pltpu.SemaphoreType.REGULAR((3,)),
            pltpu.SemaphoreType.REGULAR((2,)),
        ],
        compiler_params=pltpu.CompilerParams(
            collective_id=0, has_side_effects=True
        ),
        name="spanned_attention",
    )(
        queries, cache_keys, cache_values,
        new_keys.reshape(half, rows8, HD), new_values.reshape(half, rows8, HD),
        cache_fill, span_pos, destination,
    )

    def place(blocks_ref, spans_ref, out_ref, ak_ref, av_ref, rows, spans_here, taken, given):
        def columns(ref, h):
            return ref.at[:, pl.ds(h * GROUP * HD, GROUP * HD)]

        moves = [
            (blocks_ref.at[h], columns(rows, h), columns(rows, h), columns(out_ref, h)) for h in range(n_kvh)
        ]
        for part, target in ((0, ak_ref), (half, av_ref)):
            some = pl.ds(part, half)
            moves.append((spans_ref.at[some], spans_here.at[some], spans_here.at[some], target))
        takes = [pltpu.make_async_copy(m[0], m[1], taken.at[i]) for i, m in enumerate(moves)]
        gives = [pltpu.make_async_copy(m[2], m[3], given.at[i]) for i, m in enumerate(moves)]
        for copy in takes:
            copy.start()
        for take, give in zip(takes, gives):
            take.wait()
            give.start()
        for copy in gives:
            copy.wait()

    anywhere = pl.BlockSpec(memory_space=pl.ANY)
    attn, keys, values = pl.pallas_call(
        place,
        out_shape=(
            jax.ShapeDtypeStruct((SPAN // n_kvh, n_kvh * GROUP * HD), BF),
            jax.ShapeDtypeStruct((half, rows8, HD), BF),
            jax.ShapeDtypeStruct((half, rows8, HD), BF),
        ),
        in_specs=[anywhere] * 2,
        out_specs=(anywhere,) * 3,
        scratch_shapes=[
            pltpu.VMEM((SPAN // n_kvh, n_kvh * GROUP * HD), BF),
            pltpu.VMEM((pieces, rows8, HD), BF),
            dma((n_kvh + 2,)),
            dma((n_kvh + 2,)),
        ],
        name="place_outputs",
    )(blocks, spans)
    return attn, keys.reshape(SPAN, HD), values.reshape(SPAN, HD)


def solution(mesh):
    placed = (
        P("ctx", "kvh"),
        P("ctx", "kvh"),
        P("ctx", "kvh"),
        P("ctx", "kvh"),
        P("ctx", "kvh"),
        P(),
        P("ctx"),
        P(),
    )
    return jax.shard_map(
        per_device,
        mesh=mesh,
        in_specs=placed,
        out_specs=(P(("ctx", "kvh"), None), P("ctx", "kvh"), P("ctx", "kvh")),
        check_vma=False,
    )
```

time: 42.2 us -> 36.7 us (0.87)
  Pallas kernels: 40.8 us -> 35.2 us
    pallas_call x1, Pallas kernels: 39.1 us -> 33.5 us  [per_device(): pl.pallas_call(kernel, out_shape=(jax.ShapeDtypeStruct((n_kvh, SPAN // n_...]
where the time goes in v3:
time: 36.7 us; the launch traced here: 36.5 us
  Pallas kernels  35.2 us (96%)
  between operations  1.29 us (4%)
    pallas_call x1, Pallas kernels, per_device(): pl.pallas_call(kernel, out_shape=(jax.ShapeDtypeStruct((n_kvh, SPAN // n_...  33.5 us
    pallas_call x1, Pallas kernels, per_device(): pl.pallas_call(place, out_shape=(jax.ShapeDtypeStruct((SPAN // n_kvh, n_k...  1.7 us

profile of v3, /device:TPU:8, one launch (start us, length us, event | category | flops | bytes accessed | tf_op | source)
XLA Modules:
  0.0 36.5 jit_solution(12556367873904805473)
XLA Ops:
  1.3 33.5 %spanned_attention.1 = (bf16[8,16,1024]{2,1,0:T(8,128)(2,1)}, bf16[32,8,128]{2,1,0:T(8,128)(2,1)}) custom-call(bf16[128,1024]{1,0:T(8,128)(2,1)} %q_hbm.1, bf16[512,128]{1,0:T(8,128)(2,1)} %ck_hbm.1, bf16[512,128]{1,0:T(8,128)(2,1)} %cv_hbm.1, bf16[16,8,128]{2,1,0:T(8,128)(2,1)} %bitcast.4, bf16[16,8,128]{2,1,0:T(8,128)(2,1)} %bitcast.5, s32[32]{0:T(128)} %fill_hbm.1, ...), custom_call_target="tpu_custom_call" | custom-call | tf_op jit(solution)/shard_map/spanned_attention/pallas_call | solution.py:427
  34.8 1.7 %place_outputs.1 = (bf16[16,8192]{1,0:T(8,128)(2,1)}, bf16[16,8,128]{2,1,0:T(8,128)(2,1)}, bf16[16,8,128]{2,1,0:T(8,128)(2,1)}) custom-call(bf16[8,16,1024]{2,1,0:T(8,128)(2,1)} %get-tuple-element.8.blocks_ref, bf16[32,8,128]{2,1,0:T(8,128)(2,1)} %get-tuple-element.9.spans_ref), custom_call_target="tpu_custom_call" | custom-call | tf_op jit(solution)/shard_map/place_outputs/pallas_call | solution.py:496

commit v4 on v3

--- a/solution.py
+++ b/solution.py
@@ -30,9 +30,9 @@
 )
 SEQ = (
     (
-        ((2, 0), (0, 0, 0, 0, 1), (1, 0, 0, 0, 1, 0, 2), (1, 0, 0, 0, 1, 0, 1), (5, 0), (2, 1), (0, 1, 0, 1, 1), (1, 1, 0, 1, 1, 0, 1), (0, 1, 0, 0, 1), (0, 0, 0, 1, 1)),
+        ((2, 0), (0, 0, 0, 0, 1), (1, 0, 0, 0, 1, 0, 2), (1, 0, 0, 0, 1, 0, 1), (2, 1), (5, 0), (2, 2), (3,), (0, 1, 0, 1, 1), (1, 1, 0, 1, 1, 0, 1), (0, 1, 0, 0, 1), (0, 0, 0, 1, 1)),
         ((0, 0, 3, 1, 1), (0, 1, 3, 0, 1), (0, 0, 3, 0, 1), (0, 1, 3, 1, 1)),
-        ((0, 1, 2, 0, 1), (0, 1, 2, 1, 1), (2, 2), (3,), (5, 1), (0, 0, 2, 1, 1), (0, 0, 2, 0, 1)),
+        ((0, 1, 2, 0, 1), (0, 1, 2, 1, 1), (5, 1), (0, 0, 2, 1, 1), (0, 0, 2, 0, 1)),
         ((0, 0, 3, 1, 2), (0, 0, 3, 0, 2), (0, 1, 3, 0, 2), (0, 1, 3, 1, 2)),
         ((0, 1, 1, 0, 1), (0, 1, 1, 1, 1), (0, 0, 1, 1, 1), (0, 0, 1, 0, 1)),
         ((0, 1, 2, 0, 2), (0, 1, 2, 1, 2), (0, 0, 2, 1, 2), (0, 0, 2, 0, 2)),
@@ -40,16 +40,16 @@
     ),
     (
         ((0, 1, 0, 0, 0), (0, 1, 0, 1, 0), (0, 0, 0, 0, 0), (0, 0, 0, 1, 0)),
-        ((0, 1, 1, 0, 1), (1, 1, 1, 0, 1, 0, 3), (1, 1, 1, 0, 1, 0, 0), (0, 0, 3, 1, 0), (1, 0, 3, 1, 0, 1, 1), (2, 0), (0, 0, 3, 0, 0), (1, 0, 3, 0, 0, 1, 1), (0, 1, 0, 0, 1), (1, 1, 0, 0, 1, 0, 0), (1, 1, 0, 0, 1, 0, 3), (0, 1, 3, 1, 0), (1, 1, 3, 1, 0, 1, 1), (5, 0), (0, 0, 0, 1, 1), (1, 0, 0, 1, 1, 0, 0), (0, 0, 3, 1, 1), (1, 0, 3, 1, 1, 1, 1), (1, 0, 3, 1, 1, 0, 3), (1, 0, 3, 1, 1, 0, 0), (0, 1, 3, 0, 1), (1, 1, 3, 0, 1, 0, 0), (2, 1), (0, 0, 3, 0, 1), (1, 0, 3, 0, 1, 0, 3), (1, 0, 3, 0, 1, 1, 1), (1, 0, 3, 0, 1, 0, 0), (0, 1, 2, 0, 1), (1, 1, 2, 0, 1, 0, 0), (1, 1, 2, 0, 1, 1, 1), (0, 1, 3, 1, 1), (1, 1, 3, 1, 1, 1, 1), (1, 1, 3, 1, 1, 0, 3), (1, 1, 3, 1, 1, 0, 0), (0, 1, 2, 1, 1), (1, 1, 2, 1, 1, 0, 0), (1, 1, 2, 1, 1, 1, 1)),
+        ((2, 0), (0, 1, 1, 0, 1), (1, 1, 1, 0, 1, 0, 3), (1, 1, 1, 0, 1, 0, 0), (0, 0, 3, 1, 0), (1, 0, 3, 1, 0, 1, 1), (0, 0, 3, 0, 0), (1, 0, 3, 0, 0, 1, 1), (0, 1, 0, 0, 1), (1, 1, 0, 0, 1, 0, 0), (1, 1, 0, 0, 1, 0, 3), (2, 1), (0, 1, 3, 1, 0), (1, 1, 3, 1, 0, 1, 1), (5, 0), (0, 0, 0, 1, 1), (1, 0, 0, 1, 1, 0, 0), (0, 0, 3, 1, 1), (1, 0, 3, 1, 1, 1, 1), (1, 0, 3, 1, 1, 0, 3), (1, 0, 3, 1, 1, 0, 0), (0, 1, 3, 0, 1), (1, 1, 3, 0, 1, 0, 0), (2, 2), (3,), (0, 0, 3, 0, 1), (1, 0, 3, 0, 1, 0, 3), (1, 0, 3, 0, 1, 1, 1), (1, 0, 3, 0, 1, 0, 0), (0, 1, 2, 0, 1), (1, 1, 2, 0, 1, 0, 0), (1, 1, 2, 0, 1, 1, 1), (0, 1, 3, 1, 1), (1, 1, 3, 1, 1, 1, 1), (1, 1, 3, 1, 1, 0, 3), (1, 1, 3, 1, 1, 0, 0), (0, 1, 2, 1, 1), (1, 1, 2, 1, 1, 0, 0), (1, 1, 2, 1, 1, 1, 1)),
         ((0, 0, 3, 1, 2), (1, 0, 3, 1, 2, 0, 2), (1, 0, 3, 1, 2, 0, 0), (0, 0, 2, 1, 1), (1, 0, 2, 1, 1, 1, 1), (1, 0, 2, 1, 1, 0, 0), (0, 0, 0, 0, 1), (0, 1, 0, 1, 1)),
-        ((0, 0, 3, 0, 2), (1, 0, 3, 0, 2, 0, 0), (0, 1, 3, 0, 2), (1, 1, 3, 0, 2, 0, 0), (2, 2), (3,), (5, 1), (0, 1, 2, 0, 2), (1, 1, 2, 0, 2, 0, 0), (0, 0, 2, 0, 1), (1, 0, 2, 0, 1, 0, 0), (1, 0, 2, 0, 1, 1, 1)),
+        ((0, 0, 3, 0, 2), (1, 0, 3, 0, 2, 0, 0), (0, 1, 3, 0, 2), (1, 1, 3, 0, 2, 0, 0), (5, 1), (0, 1, 2, 0, 2), (1, 1, 2, 0, 2, 0, 0), (0, 0, 2, 0, 1), (1, 0, 2, 0, 1, 0, 0), (1, 0, 2, 0, 1, 1, 1)),
         ((0, 1, 3, 1, 2), (1, 1, 3, 1, 2, 0, 2), (1, 1, 3, 1, 2, 0, 0), (0, 1, 1, 1, 1), (1, 1, 1, 1, 1, 0, 0), (1, 1, 1, 1, 1, 1, 0)),
         ((0, 1, 2, 1, 2), (1, 1, 2, 1, 2, 0, 0), (0, 0, 1, 1, 1), (1, 0, 1, 1, 1, 0, 0), (0, 0, 2, 1, 2), (1, 0, 2, 1, 2, 0, 0), (0, 0, 1, 0, 1), (1, 0, 1, 0, 1, 0, 0), (1, 0, 1, 0, 1, 1, 0)),
         ((0, 0, 2, 0, 2), (1, 0, 2, 0, 2, 0, 0)),
     ),
     (
-        ((2, 0), (5, 0), (2, 1), (0, 1, 0, 1, 0), (1, 1, 0, 1, 0, 0, 3), (1, 1, 0, 1, 0, 1, 2), (0, 1, 2, 0, 1), (0, 1, 2, 1, 1), (0, 0, 2, 1, 1), (0, 0, 2, 0, 1)),
-        ((2, 2), (3,), (0, 0, 0, 0, 0), (1, 0, 0, 0, 0, 0, 3), (0, 1, 0, 0, 0), (0, 0, 0, 1, 0)),
+        ((2, 0), (2, 1), (5, 0), (2, 2), (3,), (0, 1, 0, 1, 0), (1, 1, 0, 1, 0, 0, 3), (1, 1, 0, 1, 0, 1, 2), (0, 1, 2, 0, 1), (0, 1, 2, 1, 1), (0, 0, 2, 1, 1), (0, 0, 2, 0, 1)),
+        ((0, 0, 0, 0, 0), (1, 0, 0, 0, 0, 0, 3), (0, 1, 0, 0, 0), (0, 0, 0, 1, 0)),
         ((0, 1, 1, 1, 0), (0, 0, 1, 1, 0), (0, 0, 1, 0, 0), (5, 1), (0, 1, 1, 0, 0)),
         ((0, 0, 0, 0, 1), (1, 0, 0, 0, 1, 0, 3), (0, 1, 1, 1, 1), (0, 0, 1, 1, 1), (0, 0, 1, 0, 1), (0, 1, 1, 0, 1)),
         ((0, 1, 0, 1, 1), (1, 1, 0, 1, 1, 0, 3), (0, 0, 0, 1, 1), (0, 1, 0, 0, 1)),
@@ -58,9 +58,9 @@
     ),
     (
         ((0, 1, 2, 1, 0), (0, 0, 2, 1, 0), (0, 1, 2, 0, 0), (0, 0, 2, 0, 0)),
-        ((0, 1, 3, 0, 1), (1, 1, 3, 0, 1, 1, 3), (1, 1, 3, 0, 1, 0, 1), (1, 1, 3, 0, 1, 0, 2), (2, 0), (0, 1, 2, 0, 1), (1, 1, 2, 0, 1, 0, 2), (1, 1, 2, 0, 1, 0, 1), (0, 1, 1, 1, 0), (1, 1, 1, 1, 0, 1, 3), (1, 1, 1, 1, 0, 0, 2), (0, 1, 2, 1, 1), (1, 1, 2, 1, 1, 0, 1), (1, 1, 2, 1, 1, 0, 2), (0, 1, 0, 0, 0), (1, 1, 0, 0, 0, 0, 2), (5, 0), (0, 0, 2, 1, 1), (1, 0, 2, 1, 1, 0, 1), (1, 0, 2, 1, 1, 0, 2), (0, 0, 1, 1, 0), (1, 0, 1, 1, 0, 1, 3), (1, 0, 1, 1, 0, 0, 2), (0, 0, 0, 1, 0), (1, 0, 0, 1, 0, 0, 2), (1, 0, 0, 1, 0, 1, 3), (0, 1, 3, 0, 2), (1, 1, 3, 0, 2, 0, 1), (1, 1, 3, 0, 2, 0, 2), (2, 1), (0, 0, 2, 0, 1), (1, 0, 2, 0, 1, 0, 1), (1, 0, 2, 0, 1, 0, 2), (0, 1, 1, 1, 1), (1, 1, 1, 1, 1, 0, 2), (1, 1, 1, 1, 1, 0, 1), (0, 0, 1, 0, 0), (1, 0, 1, 0, 0, 0, 2), (1, 0, 1, 0, 0, 1, 3)),
+        ((2, 0), (0, 1, 3, 0, 1), (1, 1, 3, 0, 1, 1, 3), (1, 1, 3, 0, 1, 0, 1), (1, 1, 3, 0, 1, 0, 2), (0, 1, 2, 0, 1), (1, 1, 2, 0, 1, 0, 2), (1, 1, 2, 0, 1, 0, 1), (0, 1, 1, 1, 0), (1, 1, 1, 1, 0, 1, 3), (1, 1, 1, 1, 0, 0, 2), (0, 1, 2, 1, 1), (1, 1, 2, 1, 1, 0, 1), (1, 1, 2, 1, 1, 0, 2), (2, 1), (0, 1, 0, 0, 0), (1, 1, 0, 0, 0, 0, 2), (5, 0), (0, 0, 2, 1, 1), (1, 0, 2, 1, 1, 0, 1), (1, 0, 2, 1, 1, 0, 2), (0, 0, 1, 1, 0), (1, 0, 1, 1, 0, 1, 3), (1, 0, 1, 1, 0, 0, 2), (0, 0, 0, 1, 0), (1, 0, 0, 1, 0, 0, 2), (1, 0, 0, 1, 0, 1, 3), (0, 1, 3, 0, 2), (1, 1, 3, 0, 2, 0, 1), (1, 1, 3, 0, 2, 0, 2), (2, 2), (3,), (0, 0, 2, 0, 1), (1, 0, 2, 0, 1, 0, 1), (1, 0, 2, 0, 1, 0, 2), (0, 1, 1, 1, 1), (1, 1, 1, 1, 1, 0, 2), (1, 1, 1, 1, 1, 0, 1), (0, 0, 1, 0, 0), (1, 0, 1, 0, 0, 0, 2), (1, 0, 1, 0, 0, 1, 3)),
         ((0, 0, 1, 1, 1), (1, 0, 1, 1, 1, 0, 1), (1, 0, 1, 1, 1, 1, 3), (1, 0, 1, 1, 1, 0, 2), (0, 0, 0, 1, 1), (1, 0, 0, 1, 1, 0, 2), (0, 1, 1, 0, 0), (1, 1, 1, 0, 0, 0, 2)),
-        ((0, 0, 1, 0, 1), (1, 0, 1, 0, 1, 0, 1), (1, 0, 1, 0, 1, 0, 2), (2, 2), (3,), (5, 1), (0, 1, 1, 0, 1), (1, 1, 1, 0, 1, 1, 3), (1, 1, 1, 0, 1, 0, 2)),
+        ((0, 0, 1, 0, 1), (1, 0, 1, 0, 1, 0, 1), (1, 0, 1, 0, 1, 0, 2), (5, 1), (0, 1, 1, 0, 1), (1, 1, 1, 0, 1, 1, 3), (1, 1, 1, 0, 1, 0, 2)),
         ((0, 0, 1, 1, 2), (1, 0, 1, 1, 2, 0, 0), (0, 1, 0, 0, 1), (1, 1, 0, 0, 1, 0, 2), (0, 1, 0, 1, 0), (0, 0, 0, 0, 0)),
         ((0, 0, 3, 1, 1), (1, 0, 3, 1, 1, 0, 2), (0, 1, 1, 0, 2), (1, 1, 1, 0, 2, 0, 0), (0, 0, 3, 0, 1), (1, 0, 3, 0, 1, 0, 2), (1, 0, 3, 0, 1, 1, 2), (0, 1, 3, 1, 1), (1, 1, 3, 1, 1, 0, 2)),
         ((0, 0, 0, 0, 1), (0, 1, 0, 1, 1)),
@@ -249,7 +249,7 @@
                     parts.append(s)
             return parts
 
-        def shard_absorb(slots, tile, parts):
+        def shard_absorb(slots, final, tile, parts):
             lanes = lanes_of(tile)
             old = m_ref[:, lanes]
             top = jnp.maximum(old, jnp.max(functools.reduce(jnp.maximum, parts), axis=0, keepdims=True))
@@ -257,6 +257,8 @@
             for i, part in enumerate(parts):
                 weights = jnp.exp2((part - top) * scaling).astype(BF)
                 total = total + dot(vb[slots[i // 2] * 2 + i % 2], weights)
+            if final:
+                return total
             acc[:, lanes] = total
             m_ref[:, lanes] = top
 
@@ -265,15 +267,15 @@
             for i, tile in enumerate(order):
                 if i + depth < len(order):
                     ahead.append(scores(order[i + depth]))
-                absorb(tile, ahead.pop(0))
+                total = absorb(tile, ahead.pop(0))
                 if after is not None:
-                    after(i, tile)
+                    after(i, tile, total)
 
         def attend(slots, home=False, order=tuple(range(tiles)), after=None):
             in_turn(
                 order,
                 functools.partial(shard_scores, slots, home),
-                functools.partial(shard_absorb, slots),
+                functools.partial(shard_absorb, slots, after is not None),
                 after,
                 AHEAD if len(slots) == 1 else PAIR_AHEAD,
             )
@@ -369,33 +371,28 @@
                 device_id=(me, b), device_id_type=MESH,
             )
 
-        def ship(tile):
-            for half in range(2):
-                b = tile * 2 + half
-
-                @pl.when(b != head)
-                def _():
-                    out_copy(b).start()
-
-                @pl.when(b == head)
-                def _():
-                    pltpu.make_async_copy(obuf.at[b], arecv.at[b], home.at[0]).start()
+        def ship(i):
+            if i < tiles - 1:
+                for part in range(2):
+                    out_copy(turn[i] * 2 + part).start()
+            else:
+                out_copy(head ^ 1).start()
+                pltpu.make_async_copy(obuf.at[head], arecv.at[head], home.at[0]).start()
 
         turn = [lax.rem(head // 2 + i, tiles) for i in (2, 1, 3, 0)]
 
-        def finish(i, tile):
-            lanes = lanes_of(tile)
-            result = acc[0:HD, lanes] * (1.0 / acc[HD:HD + 1, lanes])
+        def finish(i, tile, total):
+            result = total[0:HD] * (1.0 / total[HD:HD + 1])
             result = result.T.astype(BF)
             for part in range(2):
                 for g in range(GROUP):
                     at_row = part * 128 + g * 16
                     obuf[tile * 2 + part, :, g * HD:(g + 1) * HD] = result[at_row:at_row + 16]
             if i > 0:
-                ship(turn[i - 1])
+                ship(i - 1)
 
         attend(last, order=turn, after=finish)
-        ship(turn[-1])
+        ship(tiles - 1)
         if STAGE_TWO == 7:
             stage_two()
 
@@ -442,8 +439,8 @@
             pltpu.SMEM((n_ctx,), jnp.int32),
             pltpu.SMEM((n_ctx,), jnp.int32),
             pltpu.VMEM((HD, GROUP * SPAN), BF),
-            pltpu.VMEM((24, HALF, HD), BF),
-            pltpu.VMEM((24, VROWS, HALF), BF),
+            pltpu.VMEM((32, HALF, HD), BF),
+            pltpu.VMEM((32, VROWS, HALF), BF),
             pltpu.VMEM((VROWS, SPAN), BF),
             pltpu.VMEM((VROWS, GROUP * SPAN), F32),
             pltpu.VMEM((1, GROUP * SPAN), F32),

time: 36.7 us -> 36.7 us (level)
  no operation moved by 1% of the time
where the time goes in v4:
time: 36.7 us; the launch traced here: 36.5 us
  Pallas kernels  35.3 us (96%)
  between operations  1.29 us (4%)
    pallas_call x1, Pallas kernels, per_device(): pl.pallas_call(kernel, out_shape=(jax.ShapeDtypeStruct((n_kvh, SPAN // n_...  33.6 us
    pallas_call x1, Pallas kernels, per_device(): pl.pallas_call(place, out_shape=(jax.ShapeDtypeStruct((SPAN // n_kvh, n_k...  1.7 us

profile of v4, /device:TPU:8, one launch (start us, length us, event | category | flops | bytes accessed | tf_op | source)
XLA Modules:
  0.0 36.5 jit_solution(9080769135848258909)
XLA Ops:
  1.3 33.6 %spanned_attention.1 = (bf16[8,16,1024]{2,1,0:T(8,128)(2,1)}, bf16[32,8,128]{2,1,0:T(8,128)(2,1)}) custom-call(bf16[128,1024]{1,0:T(8,128)(2,1)} %q_hbm.1, bf16[512,128]{1,0:T(8,128)(2,1)} %ck_hbm.1, bf16[512,128]{1,0:T(8,128)(2,1)} %cv_hbm.1, bf16[16,8,128]{2,1,0:T(8,128)(2,1)} %bitcast.4, bf16[16,8,128]{2,1,0:T(8,128)(2,1)} %bitcast.5, s32[32]{0:T(128)} %fill_hbm.1, ...), custom_call_target="tpu_custom_call" | custom-call | tf_op jit(solution)/shard_map/spanned_attention/pallas_call | solution.py:424
  34.8 1.7 %place_outputs.1 = (bf16[16,8192]{1,0:T(8,128)(2,1)}, bf16[16,8,128]{2,1,0:T(8,128)(2,1)}, bf16[16,8,128]{2,1,0:T(8,128)(2,1)}) custom-call(bf16[8,16,1024]{2,1,0:T(8,128)(2,1)} %get-tuple-element.8.blocks_ref, bf16[32,8,128]{2,1,0:T(8,128)(2,1)} %get-tuple-element.9.spans_ref), custom_call_target="tpu_custom_call" | custom-call | tf_op jit(solution)/shard_map/place_outputs/pallas_call | solution.py:493

commit v5 on v4

--- a/solution.py
+++ b/solution.py
@@ -396,16 +396,6 @@
         if STAGE_TWO == 7:
             stage_two()
 
-        for k in range(1, n_kvh):
-            h = lax.rem(head + k, n_kvh)
-            pltpu.make_async_remote_copy(
-                src_ref=obuf.at[h], dst_ref=arecv.at[h], send_sem=a_s.at[h], recv_sem=a_r.at[h],
-                device_id=(me, h), device_id_type=MESH,
-            ).wait()
-        stage_wait(w2, app, 1)
-        pltpu.make_async_copy(obuf.at[head], arecv.at[head], home.at[0]).wait()
-        pltpu.make_async_copy(w2.at[me], app.at[me], home.at[1]).wait()
-
         for r in range(4):
             @pl.when(role == r)
             def _(r=r):
@@ -417,6 +407,16 @@
                         src_ref=whole, dst_ref=whole, send_sem=ss.at[t], recv_sem=rs.at[0, 0, 0],
                         device_id=at(0, role ^ 1), device_id_type=MESH,
                     ).wait_send()
+
+        for k in range(1, n_kvh):
+            h = lax.rem(head + k, n_kvh)
+            pltpu.make_async_remote_copy(
+                src_ref=obuf.at[h], dst_ref=arecv.at[h], send_sem=a_s.at[h], recv_sem=a_r.at[h],
+                device_id=(me, h), device_id_type=MESH,
+            ).wait()
+        stage_wait(w2, app, 1)
+        pltpu.make_async_copy(obuf.at[head], arecv.at[head], home.at[0]).wait()
+        pltpu.make_async_copy(w2.at[me], app.at[me], home.at[1]).wait()
 
     half = pieces // 2
     rows8 = SPAN // half

time: 36.7 us -> 36.7 us (level)
  no operation moved by 1% of the time
where the time goes in v5:
time: 36.7 us; the launch traced here: 36.5 us
  Pallas kernels  35.3 us (96%)
  between operations  1.29 us (4%)
    pallas_call x1, Pallas kernels, per_device(): pl.pallas_call(kernel, out_shape=(jax.ShapeDtypeStruct((n_kvh, SPAN // n_...  33.6 us
    pallas_call x1, Pallas kernels, per_device(): pl.pallas_call(place, out_shape=(jax.ShapeDtypeStruct((SPAN // n_kvh, n_k...  1.7 us

profile of v5, /device:TPU:8, one launch (start us, length us, event | category | flops | bytes accessed | tf_op | source)
XLA Modules:
  0.0 36.5 jit_solution(11752843660655776530)
XLA Ops:
  1.3 33.6 %spanned_attention.1 = (bf16[8,16,1024]{2,1,0:T(8,128)(2,1)}, bf16[32,8,128]{2,1,0:T(8,128)(2,1)}) custom-call(bf16[128,1024]{1,0:T(8,128)(2,1)} %q_hbm.1, bf16[512,128]{1,0:T(8,128)(2,1)} %ck_hbm.1, bf16[512,128]{1,0:T(8,128)(2,1)} %cv_hbm.1, bf16[16,8,128]{2,1,0:T(8,128)(2,1)} %bitcast.4, bf16[16,8,128]{2,1,0:T(8,128)(2,1)} %bitcast.5, s32[32]{0:T(128)} %fill_hbm.1, ...), custom_call_target="tpu_custom_call" | custom-call | tf_op jit(solution)/shard_map/spanned_attention/pallas_call | solution.py:424
  34.8 1.7 %place_outputs.1 = (bf16[16,8192]{1,0:T(8,128)(2,1)}, bf16[16,8,128]{2,1,0:T(8,128)(2,1)}, bf16[16,8,128]{2,1,0:T(8,128)(2,1)}) custom-call(bf16[8,16,1024]{2,1,0:T(8,128)(2,1)} %get-tuple-element.8.blocks_ref, bf16[32,8,128]{2,1,0:T(8,128)(2,1)} %get-tuple-element.9.spans_ref), custom_call_target="tpu_custom_call" | custom-call | tf_op jit(solution)/shard_map/place_outputs/pallas_call | solution.py:493
